TPU v7x, 128 devices: a whole 4x4x4 slice. The times are simulated.
128 devices in a mesh: beam: 16 (over z_lo, y, core), hid: 8 (over x, z_hi).
Axes of the slice: x: 4, y: 4, z: 4 (z_hi: 2, z_lo: 2; z = z_hi * 2 + z_lo), core: 2. Of those that a mesh axis runs over, the one named last changes fastest.
Arguments:
- queries: bfloat16 [1024, 256], P('beam'), may hold values from -6 to 6
- beam_ids: int32 [1024, 256], P('beam'), may hold values from 0 to 262143, as said below
- child_table: bfloat16 [524288, 256], P('beam'), may hold values from -6 to 6
- w_query: bfloat16 [256, 1024], P(None, 'hid'), may hold values from -0.21875 to 0.21875
- w_child: bfloat16 [256, 1024], P(None, 'hid'), may hold values from -0.21875 to 0.21875
- w_cross: bfloat16 [256, 1024], P(None, 'hid'), may hold values from -0.21875 to 0.21875
- bias: float32 [1024], P('hid'), may hold values from -3 to 3
- w_out: float32 [1024], P('hid'), may hold values from -0.1875 to 0.1875
Outputs:
- scores: float32 [1024, 512], P('beam', 'hid')
Inputs may be any that keep to these rules, and one draw needn't show every extreme that they name: `beam_ids`: each id b names a node of the current level; its children are rows 2 b and 2 b + 1 of child_table. Among the ids of one index of beam's 64 queries, at most 1536 lie in the rows held by one index of beam (ids r * 16384 to (r + 1) * 16384 - 1 for index r), and in every draw one such index receives exactly 1536 from every index of beam.
All inputs are finite; a program needn't handle non-finite values.
Results may differ from a plain program's by a relative error of at most 0.0019.
Values may be sent and summed in bfloat16 or wider, within the bound.
A program may use at most 128 MiB of HBM per device.

v0:
```python
import math

import jax
import jax.numpy as jnp
from jax import lax
from jax.sharding import PartitionSpec as P


def cut_along(shard, dim, size):
    before, after = (shard.shape[:dim], shard.shape[dim + 1 :])
    return jnp.moveaxis(shard.reshape(*before, size, -1, *after), dim, 0)


def edges_of(length, count):
    hop = length // count
    if hop >= 8:
        hop -= hop % 8
    return [hop * k for k in range(1, count)]


def in_order(pieces, dim):
    pieces = jnp.moveaxis(pieces, 0, dim)
    lengths = pieces.shape
    return pieces.reshape(*lengths[:dim], lengths[dim] * lengths[dim + 1], *lengths[dim + 2 :])


def cut_exchange(shard, axis, pieces, split_dim, concat_dim):
    blocks = cut_along(shard, split_dim, lax.axis_size(axis))
    cut = max(range(1, max(2, blocks.ndim - 1)), key=lambda d: blocks.shape[d])
    gathered = []
    for share in jnp.split(blocks, edges_of(blocks.shape[cut], pieces), axis=cut):
        if share.size:
            gathered.append(lax.all_to_all(share, axis, split_axis=0, concat_axis=0, tiled=True))
    return in_order(jnp.concatenate(gathered, axis=cut), concat_dim)


def sum_at_owner(shard, axis, dim):
    size = lax.axis_size(axis)
    pieces = lax.all_to_all(cut_along(shard, dim, size), axis, 0, 0, tiled=True)
    return jnp.sum(pieces, axis=0)


def owner_ranks(owners, nbeam):
    slots = owners.shape[0]
    block = math.gcd(slots, 512)
    blocks = slots // block
    onehot = (owners[:, None] == jnp.arange(nbeam, dtype=jnp.int32)[None, :]).astype(jnp.bfloat16)
    blocked = onehot.reshape(blocks, block, nbeam)
    lower = (jnp.arange(block)[:, None] > jnp.arange(block)[None, :]).astype(jnp.bfloat16)
    inside = jnp.einsum("ij,bjn->bin", lower, blocked, preferred_element_type=jnp.float32)
    totals = jnp.sum(blocked.astype(jnp.float32), axis=1)
    before = jnp.cumsum(totals, axis=0) - totals
    counts = (inside + before[:, None, :]).reshape(slots, nbeam)
    return jnp.sum(counts * onehot.astype(jnp.float32), axis=1).astype(jnp.int32)


def place_tables(position, offsets, nbeam, capacity):
    slots = position.shape[0]
    index = jnp.arange(slots, dtype=jnp.int32)

    def per_owner(owner):
        wanted = owner * capacity + jnp.arange(capacity, dtype=jnp.int32)
        equal = wanted[:, None] == position[None, :]
        asked = jnp.sum(jnp.where(equal, offsets[None, :], 0), axis=1)
        slot_of = jnp.sum(jnp.where(equal, index[None, :], 0), axis=1)
        live = jnp.any(equal, axis=1).astype(jnp.float32)
        return (asked, slot_of, live)

    return lax.map(per_owner, jnp.arange(nbeam, dtype=jnp.int32))


def shards(queries, beam_ids, child_table, w_query, w_child, w_cross, bias, w_out):
    nbeam = lax.axis_size("beam")
    nhid = lax.axis_size("hid")
    qcount, width = beam_ids.shape
    embed = queries.shape[1]
    slots = qcount * width
    half = child_table.shape[0] // 2
    capacity = 3 * slots // (2 * nbeam)
    pairs_table = child_table.reshape(half, 2 * embed)
    flat_ids = beam_ids.reshape(slots)
    owners = flat_ids // half
    offsets = flat_ids - owners * half
    ranks = owner_ranks(owners, nbeam)
    position = owners * capacity + ranks
    requests, slot_table, live_table = place_tables(position, offsets, nbeam, capacity)
    share = capacity // nhid
    mine = lax.dynamic_slice_in_dim(requests, lax.axis_index("hid") * share, share, 1)
    found = pairs_table[lax.all_to_all(mine, "beam", split_axis=0, concat_axis=0, tiled=True)]
    gotten = cut_exchange(found, "beam", 2, 0, 0)
    fetched = lax.all_gather(gotten, "hid", axis=1, tiled=True)
    received = fetched.reshape(nbeam * capacity, 2 * embed)
    qproj = jnp.dot(queries, w_query, preferred_element_type=jnp.float32) + bias
    block = math.gcd(qcount, max(1, 1024 // width))
    blocks = qcount // block

    def score_block(packed):
        where_rows, qblock, pblock = packed
        rows = received[where_rows].reshape(block, 2 * width, embed)
        cross = (qblock[:, None, :].astype(jnp.float32) * rows.astype(jnp.float32)).astype(
            jnp.bfloat16
        )
        flat_rows = rows.reshape(block * 2 * width, embed)
        flat_cross = cross.reshape(block * 2 * width, embed)
        pre = jnp.dot(flat_rows, w_child, preferred_element_type=jnp.float32) + jnp.dot(
            flat_cross, w_cross, preferred_element_type=jnp.float32
        )
        pre = pre.reshape(block, 2 * width, -1) + pblock[:, None, :]
        return jnp.sum(jnp.maximum(pre, 0.0) * w_out, axis=-1)

    partial_scores = lax.map(
        score_block,
        (
            position.reshape(blocks, block * width),
            queries.reshape(blocks, block, embed),
            qproj.reshape(blocks, block, -1),
        ),
    )
    partial_scores = partial_scores.reshape(qcount, 2 * width)
    return sum_at_owner(partial_scores, "hid", 1)


def solution(mesh):
    return jax.shard_map(
        shards,
        mesh=mesh,
        in_specs=(
            P("beam", None),
            P("beam", None),
            P("beam", None),
            P(None, "hid"),
            P(None, "hid"),
            P(None, "hid"),
            P("hid"),
            P("hid"),
        ),
        out_specs=P("beam", "hid"),
        check_vma=False,
    )
```

profile of v0, /device:TPU:0, one launch (start us, length us, event | category | flops | bytes accessed | tf_op | source)
XLA Modules:
  0.0 969.3 jit_solution(9309029163396406707)
XLA Ops:
  6.5 0.9 reshape.187
  8.4 0.9 copy.24
  9.3 267.1 %while.20 = (s32[]{:T(128)}, s32[16,1536]{1,0:T(8,128)S(1)}, s32[16]{0:T(128)S(1)}, s32[16384]{0:T(1024)S(1)}, s32[16384]{0:T(1024)S(1)}, /*index=5*/s32[]{:T(128)}, s32[1]{0:T(128)}, s32[]{:T(128)}) while((s32[]{:T(128)}, s32[16,1536]{1,0:T(8,128)S(1)}, s32[16]{0:T(128)S(1)}, s32[16384]{0:T(1024)S(1)}, s32[16384]{0:T(1024)S(1)}, ...), condition=%wide.region_5.6_spmd, body=%wide.region_3.5_spmd.sunk | while | flops 75497472 | bytes 174205 | solution.py:69
  10.7 15.1 %select_reduce_fusion.2 = s32[1536]{0:T(1024)S(1)} fusion(s32[16384]{0:T(1024)S(1)} %get-tuple-element.266, s32[16384]{0:T(1024)S(1)} %get-tuple-element.265, s32[1536]{0:T(1024)S(1)} %iota_add_fusion.2), kind=kLoop, calls=%fused_computation.2.clone.1 | loop fusion | flops 75495936 | bytes 143360 | tf_op jit(solution)/shard_map/while/body/eval_jaxpr/reduce_sum | solution.py:64
  27.4 15.1 %select_reduce_fusion.2 = s32[1536]{0:T(1024)S(1)} fusion(s32[16384]{0:T(1024)S(1)} %get-tuple-element.266, s32[16384]{0:T(1024)S(1)} %get-tuple-element.265, s32[1536]{0:T(1024)S(1)} %iota_add_fusion.2), kind=kLoop, calls=%fused_computation.2.clone.1 | loop fusion | flops 75495936 | bytes 143360 | tf_op jit(solution)/shard_map/while/body/eval_jaxpr/reduce_sum | solution.py:64
  44.1 15.1 %select_reduce_fusion.2 = s32[1536]{0:T(1024)S(1)} fusion(s32[16384]{0:T(1024)S(1)} %get-tuple-element.266, s32[16384]{0:T(1024)S(1)} %get-tuple-element.265, s32[1536]{0:T(1024)S(1)} %iota_add_fusion.2), kind=kLoop, calls=%fused_computation.2.clone.1 | loop fusion | flops 75495936 | bytes 143360 | tf_op jit(solution)/shard_map/while/body/eval_jaxpr/reduce_sum | solution.py:64
  60.8 15.1 %select_reduce_fusion.2 = s32[1536]{0:T(1024)S(1)} fusion(s32[16384]{0:T(1024)S(1)} %get-tuple-element.266, s32[16384]{0:T(1024)S(1)} %get-tuple-element.265, s32[1536]{0:T(1024)S(1)} %iota_add_fusion.2), kind=kLoop, calls=%fused_computation.2.clone.1 | loop fusion | flops 75495936 | bytes 143360 | tf_op jit(solution)/shard_map/while/body/eval_jaxpr/reduce_sum | solution.py:64
  77.5 15.1 %select_reduce_fusion.2 = s32[1536]{0:T(1024)S(1)} fusion(s32[16384]{0:T(1024)S(1)} %get-tuple-element.266, s32[16384]{0:T(1024)S(1)} %get-tuple-element.265, s32[1536]{0:T(1024)S(1)} %iota_add_fusion.2), kind=kLoop, calls=%fused_computation.2.clone.1 | loop fusion | flops 75495936 | bytes 143360 | tf_op jit(solution)/shard_map/while/body/eval_jaxpr/reduce_sum | solution.py:64
  94.2 15.1 %select_reduce_fusion.2 = s32[1536]{0:T(1024)S(1)} fusion(s32[16384]{0:T(1024)S(1)} %get-tuple-element.266, s32[16384]{0:T(1024)S(1)} %get-tuple-element.265, s32[1536]{0:T(1024)S(1)} %iota_add_fusion.2), kind=kLoop, calls=%fused_computation.2.clone.1 | loop fusion | flops 75495936 | bytes 143360 | tf_op jit(solution)/shard_map/while/body/eval_jaxpr/reduce_sum | solution.py:64
  110.9 15.1 %select_reduce_fusion.2 = s32[1536]{0:T(1024)S(1)} fusion(s32[16384]{0:T(1024)S(1)} %get-tuple-element.266, s32[16384]{0:T(1024)S(1)} %get-tuple-element.265, s32[1536]{0:T(1024)S(1)} %iota_add_fusion.2), kind=kLoop, calls=%fused_computation.2.clone.1 | loop fusion | flops 75495936 | bytes 143360 | tf_op jit(solution)/shard_map/while/body/eval_jaxpr/reduce_sum | solution.py:64
  127.6 15.1 %select_reduce_fusion.2 = s32[1536]{0:T(1024)S(1)} fusion(s32[16384]{0:T(1024)S(1)} %get-tuple-element.266, s32[16384]{0:T(1024)S(1)} %get-tuple-element.265, s32[1536]{0:T(1024)S(1)} %iota_add_fusion.2), kind=kLoop, calls=%fused_computation.2.clone.1 | loop fusion | flops 75495936 | bytes 143360 | tf_op jit(solution)/shard_map/while/body/eval_jaxpr/reduce_sum | solution.py:64
  144.3 15.1 %select_reduce_fusion.2 = s32[1536]{0:T(1024)S(1)} fusion(s32[16384]{0:T(1024)S(1)} %get-tuple-element.266, s32[16384]{0:T(1024)S(1)} %get-tuple-element.265, s32[1536]{0:T(1024)S(1)} %iota_add_fusion.2), kind=kLoop, calls=%fused_computation.2.clone.1 | loop fusion | flops 75495936 | bytes 143360 | tf_op jit(solution)/shard_map/while/body/eval_jaxpr/reduce_sum | solution.py:64
  161.0 15.1 %select_reduce_fusion.2 = s32[1536]{0:T(1024)S(1)} fusion(s32[16384]{0:T(1024)S(1)} %get-tuple-element.266, s32[16384]{0:T(1024)S(1)} %get-tuple-element.265, s32[1536]{0:T(1024)S(1)} %iota_add_fusion.2), kind=kLoop, calls=%fused_computation.2.clone.1 | loop fusion | flops 75495936 | bytes 143360 | tf_op jit(solution)/shard_map/while/body/eval_jaxpr/reduce_sum | solution.py:64
  177.7 15.1 %select_reduce_fusion.2 = s32[1536]{0:T(1024)S(1)} fusion(s32[16384]{0:T(1024)S(1)} %get-tuple-element.266, s32[16384]{0:T(1024)S(1)} %get-tuple-element.265, s32[1536]{0:T(1024)S(1)} %iota_add_fusion.2), kind=kLoop, calls=%fused_computation.2.clone.1 | loop fusion | flops 75495936 | bytes 143360 | tf_op jit(solution)/shard_map/while/body/eval_jaxpr/reduce_sum | solution.py:64
  194.4 15.1 %select_reduce_fusion.2 = s32[1536]{0:T(1024)S(1)} fusion(s32[16384]{0:T(1024)S(1)} %get-tuple-element.266, s32[16384]{0:T(1024)S(1)} %get-tuple-element.265, s32[1536]{0:T(1024)S(1)} %iota_add_fusion.2), kind=kLoop, calls=%fused_computation.2.clone.1 | loop fusion | flops 75495936 | bytes 143360 | tf_op jit(solution)/shard_map/while/body/eval_jaxpr/reduce_sum | solution.py:64
  211.0 15.1 %select_reduce_fusion.2 = s32[1536]{0:T(1024)S(1)} fusion(s32[16384]{0:T(1024)S(1)} %get-tuple-element.266, s32[16384]{0:T(1024)S(1)} %get-tuple-element.265, s32[1536]{0:T(1024)S(1)} %iota_add_fusion.2), kind=kLoop, calls=%fused_computation.2.clone.1 | loop fusion | flops 75495936 | bytes 143360 | tf_op jit(solution)/shard_map/while/body/eval_jaxpr/reduce_sum | solution.py:64
  227.7 15.1 %select_reduce_fusion.2 = s32[1536]{0:T(1024)S(1)} fusion(s32[16384]{0:T(1024)S(1)} %get-tuple-element.266, s32[16384]{0:T(1024)S(1)} %get-tuple-element.265, s32[1536]{0:T(1024)S(1)} %iota_add_fusion.2), kind=kLoop, calls=%fused_computation.2.clone.1 | loop fusion | flops 75495936 | bytes 143360 | tf_op jit(solution)/shard_map/while/body/eval_jaxpr/reduce_sum | solution.py:64
  244.4 15.1 %select_reduce_fusion.2 = s32[1536]{0:T(1024)S(1)} fusion(s32[16384]{0:T(1024)S(1)} %get-tuple-element.266, s32[16384]{0:T(1024)S(1)} %get-tuple-element.265, s32[1536]{0:T(1024)S(1)} %iota_add_fusion.2), kind=kLoop, calls=%fused_computation.2.clone.1 | loop fusion | flops 75495936 | bytes 143360 | tf_op jit(solution)/shard_map/while/body/eval_jaxpr/reduce_sum | solution.py:64
  261.1 15.1 %select_reduce_fusion.2 = s32[1536]{0:T(1024)S(1)} fusion(s32[16384]{0:T(1024)S(1)} %get-tuple-element.266, s32[16384]{0:T(1024)S(1)} %get-tuple-element.265, s32[1536]{0:T(1024)S(1)} %iota_add_fusion.2), kind=kLoop, calls=%fused_computation.2.clone.1 | loop fusion | flops 75495936 | bytes 143360 | tf_op jit(solution)/shard_map/while/body/eval_jaxpr/reduce_sum | solution.py:64
  277.1 6.0 all-to-all-start
  283.2 24.5 %reshape.188 = bf16[16384,512]{1,0:T(8,128)(2,1)} reshape(bf16[32768,256]{1,0:T(8,128)(2,1)} %param.14) | data formatting | bytes 33554432 | tf_op jit(solution)/shard_map/reshape | solution.py:80
  307.9 19.1 %gather_fusion.1 = bf16[3072,512]{1,0:T(8,128)(2,1)S(1)} fusion(bf16[16384,512]{1,0:T(8,128)(2,1)} %reshape.188, s32[3072]{0:T(1024)S(1)} %broadcast_clamp_fusion.1), kind=kCustom, calls=%fused_computation.1 | custom fusion | bytes 6303744 | tf_op jit(solution)/shard_map/gather | solution.py:89
  327.2 27.6 %all_to_all.27 = bf16[16,1,96,512]{3,2,1,0:T(8,128)(2,1)S(1)} all-to-all(bf16[16,1,96,512]{3,2,1,0:T(8,128)(2,1)S(1)} %get-tuple-element.155), channel_id=1, replica_groups=mesh['beam'=16,'hid'=8] {'beam'}, dimensions={0} | all-to-all | bytes 3145728 | tf_op jit(solution)/shard_map/all_to_all | solution.py:33
  354.8 24.7 %all_to_all.28 = bf16[16,1,96,512]{3,2,1,0:T(8,128)(2,1)S(1)} all-to-all(bf16[16,1,96,512]{3,2,1,0:T(8,128)(2,1)S(1)} %get-tuple-element.154), channel_id=1, replica_groups=mesh['beam'=16,'hid'=8] {'beam'}, dimensions={0} | all-to-all | bytes 3145728 | tf_op jit(solution)/shard_map/all_to_all | solution.py:33
  379.5 2.0 pad_maximum_fusion
  381.5 0.8 copy-done.4
  383.0 0.7 convolution_add_fusion.2
  383.8 259.6 %all-gather.3.cloned.1.call-done = bf16[16,1,1536,512]{3,2,1,0:T(8,128)(2,1)} async-done(((bf16[16,1,192,512]{3,2,1,0:T(8,128)(2,1)}), bf16[16,1,1536,512]{3,2,1,0:T(8,128)(2,1)}) %all-gather.3.cloned.1.call-update) | async-done | bytes 25165840 | tf_op jit(solution)/shard_map/all_gather | solution.py:91
  643.4 306.0 %while.21 = (s32[]{:T(128)}, f32[16,4,512]{2,1,0:T(4,128)S(1)}, s32[16,1024]{1,0:T(8,128)S(1)}, bf16[24576,512]{1,0:T(8,128)(2,1)}, bf16[256,128]{1,0:T(8,128)(2...) while((s32[]{:T(128)}, f32[16,4,512]{2,1,0:T(4,128)S(1)}, ...), condition=%wide.region_8.9_spmd, body=%wide.region_6.8_spmd.sunk | while | flops 271322112 | bytes 14893693 | solution.py:111
  644.8 15.4 %gather_fusion = bf16[1024,512]{1,0:T(8,128)(2,1)S(1)} fusion(bf16[24576,512]{1,0:T(8,128)(2,1)} %get-tuple-element.293, s32[1024]{0:T(1024)S(1)} %broadcast_clamp_fusion.3), kind=kCustom, calls=%fused_computation.clone.1 | custom fusion | bytes 2101248 | tf_op jit(solution)/shard_map/while/body/eval_jaxpr/gather | solution.py:99
  661.1 0.7 bitcast_convert_fusion.2
  663.9 15.4 %gather_fusion = bf16[1024,512]{1,0:T(8,128)(2,1)S(1)} fusion(bf16[24576,512]{1,0:T(8,128)(2,1)} %get-tuple-element.293, s32[1024]{0:T(1024)S(1)} %broadcast_clamp_fusion.3), kind=kCustom, calls=%fused_computation.clone.1 | custom fusion | bytes 2101248 | tf_op jit(solution)/shard_map/while/body/eval_jaxpr/gather | solution.py:99
  680.2 0.7 bitcast_convert_fusion.2
  683.1 15.4 %gather_fusion = bf16[1024,512]{1,0:T(8,128)(2,1)S(1)} fusion(bf16[24576,512]{1,0:T(8,128)(2,1)} %get-tuple-element.293, s32[1024]{0:T(1024)S(1)} %broadcast_clamp_fusion.3), kind=kCustom, calls=%fused_computation.clone.1 | custom fusion | bytes 2101248 | tf_op jit(solution)/shard_map/while/body/eval_jaxpr/gather | solution.py:99
  699.4 0.7 bitcast_convert_fusion.2
  702.2 15.4 %gather_fusion = bf16[1024,512]{1,0:T(8,128)(2,1)S(1)} fusion(bf16[24576,512]{1,0:T(8,128)(2,1)} %get-tuple-element.293, s32[1024]{0:T(1024)S(1)} %broadcast_clamp_fusion.3), kind=kCustom, calls=%fused_computation.clone.1 | custom fusion | bytes 2101248 | tf_op jit(solution)/shard_map/while/body/eval_jaxpr/gather | solution.py:99
  718.5 0.7 bitcast_convert_fusion.2
  721.3 15.4 %gather_fusion = bf16[1024,512]{1,0:T(8,128)(2,1)S(1)} fusion(bf16[24576,512]{1,0:T(8,128)(2,1)} %get-tuple-element.293, s32[1024]{0:T(1024)S(1)} %broadcast_clamp_fusion.3), kind=kCustom, calls=%fused_computation.clone.1 | custom fusion | bytes 2101248 | tf_op jit(solution)/shard_map/while/body/eval_jaxpr/gather | solution.py:99
  737.6 0.7 bitcast_convert_fusion.2
  740.5 15.4 %gather_fusion = bf16[1024,512]{1,0:T(8,128)(2,1)S(1)} fusion(bf16[24576,512]{1,0:T(8,128)(2,1)} %get-tuple-element.293, s32[1024]{0:T(1024)S(1)} %broadcast_clamp_fusion.3), kind=kCustom, calls=%fused_computation.clone.1 | custom fusion | bytes 2101248 | tf_op jit(solution)/shard_map/while/body/eval_jaxpr/gather | solution.py:99
  756.7 0.7 bitcast_convert_fusion.2
  759.5 15.4 %gather_fusion = bf16[1024,512]{1,0:T(8,128)(2,1)S(1)} fusion(bf16[24576,512]{1,0:T(8,128)(2,1)} %get-tuple-element.293, s32[1024]{0:T(1024)S(1)} %broadcast_clamp_fusion.3), kind=kCustom, calls=%fused_computation.clone.1 | custom fusion | bytes 2101248 | tf_op jit(solution)/shard_map/while/body/eval_jaxpr/gather | solution.py:99
  775.8 0.7 bitcast_convert_fusion.2
  778.7 15.4 %gather_fusion = bf16[1024,512]{1,0:T(8,128)(2,1)S(1)} fusion(bf16[24576,512]{1,0:T(8,128)(2,1)} %get-tuple-element.293, s32[1024]{0:T(1024)S(1)} %broadcast_clamp_fusion.3), kind=kCustom, calls=%fused_computation.clone.1 | custom fusion | bytes 2101248 | tf_op jit(solution)/shard_map/while/body/eval_jaxpr/gather | solution.py:99
  794.9 0.7 bitcast_convert_fusion.2
  797.8 15.4 %gather_fusion = bf16[1024,512]{1,0:T(8,128)(2,1)S(1)} fusion(bf16[24576,512]{1,0:T(8,128)(2,1)} %get-tuple-element.293, s32[1024]{0:T(1024)S(1)} %broadcast_clamp_fusion.3), kind=kCustom, calls=%fused_computation.clone.1 | custom fusion | bytes 2101248 | tf_op jit(solution)/shard_map/while/body/eval_jaxpr/gather | solution.py:99
  814.1 0.7 bitcast_convert_fusion.2
  816.9 15.4 %gather_fusion = bf16[1024,512]{1,0:T(8,128)(2,1)S(1)} fusion(bf16[24576,512]{1,0:T(8,128)(2,1)} %get-tuple-element.293, s32[1024]{0:T(1024)S(1)} %broadcast_clamp_fusion.3), kind=kCustom, calls=%fused_computation.clone.1 | custom fusion | bytes 2101248 | tf_op jit(solution)/shard_map/while/body/eval_jaxpr/gather | solution.py:99
  833.2 0.7 bitcast_convert_fusion.2
  836.0 15.4 %gather_fusion = bf16[1024,512]{1,0:T(8,128)(2,1)S(1)} fusion(bf16[24576,512]{1,0:T(8,128)(2,1)} %get-tuple-element.293, s32[1024]{0:T(1024)S(1)} %broadcast_clamp_fusion.3), kind=kCustom, calls=%fused_computation.clone.1 | custom fusion | bytes 2101248 | tf_op jit(solution)/shard_map/while/body/eval_jaxpr/gather | solution.py:99
  852.3 0.7 bitcast_convert_fusion.2
  855.1 15.4 %gather_fusion = bf16[1024,512]{1,0:T(8,128)(2,1)S(1)} fusion(bf16[24576,512]{1,0:T(8,128)(2,1)} %get-tuple-element.293, s32[1024]{0:T(1024)S(1)} %broadcast_clamp_fusion.3), kind=kCustom, calls=%fused_computation.clone.1 | custom fusion | bytes 2101248 | tf_op jit(solution)/shard_map/while/body/eval_jaxpr/gather | solution.py:99
  871.4 0.7 bitcast_convert_fusion.2
  874.2 15.4 %gather_fusion = bf16[1024,512]{1,0:T(8,128)(2,1)S(1)} fusion(bf16[24576,512]{1,0:T(8,128)(2,1)} %get-tuple-element.293, s32[1024]{0:T(1024)S(1)} %broadcast_clamp_fusion.3), kind=kCustom, calls=%fused_computation.clone.1 | custom fusion | bytes 2101248 | tf_op jit(solution)/shard_map/while/body/eval_jaxpr/gather | solution.py:99
  890.5 0.7 bitcast_convert_fusion.2
  892.0 0.7 constant_dynamic-slice_fusion.3
  893.4 15.4 %gather_fusion = bf16[1024,512]{1,0:T(8,128)(2,1)S(1)} fusion(bf16[24576,512]{1,0:T(8,128)(2,1)} %get-tuple-element.293, s32[1024]{0:T(1024)S(1)} %broadcast_clamp_fusion.3), kind=kCustom, calls=%fused_computation.clone.1 | custom fusion | bytes 2101248 | tf_op jit(solution)/shard_map/while/body/eval_jaxpr/gather | solution.py:99
  909.7 0.7 bitcast_convert_fusion.2
  912.5 15.4 %gather_fusion = bf16[1024,512]{1,0:T(8,128)(2,1)S(1)} fusion(bf16[24576,512]{1,0:T(8,128)(2,1)} %get-tuple-element.293, s32[1024]{0:T(1024)S(1)} %broadcast_clamp_fusion.3), kind=kCustom, calls=%fused_computation.clone.1 | custom fusion | bytes 2101248 | tf_op jit(solution)/shard_map/while/body/eval_jaxpr/gather | solution.py:99
  928.8 0.7 bitcast_convert_fusion.2
  931.7 15.4 %gather_fusion = bf16[1024,512]{1,0:T(8,128)(2,1)S(1)} fusion(bf16[24576,512]{1,0:T(8,128)(2,1)} %get-tuple-element.293, s32[1024]{0:T(1024)S(1)} %broadcast_clamp_fusion.3), kind=kCustom, calls=%fused_computation.clone.1 | custom fusion | bytes 2101248 | tf_op jit(solution)/shard_map/while/body/eval_jaxpr/gather | solution.py:99
  947.9 0.7 bitcast_convert_fusion.2
  949.8 10.5 %all_to_all.29 = f32[8,1,4096]{2,1,0:T(1,128)S(1)} all-to-all(f32[8,1,4096]{2,1,0:T(1,128)S(1)} %reshape.218), channel_id=1, replica_groups=mesh['beam'=16,'hid'=8] {'hid'}, dimensions={0} | all-to-all | bytes 262144 | tf_op jit(solution)/shard_map/all_to_all | solution.py:39
  960.8 1.0 reduce.4
  (300 shorter events, 64.6 us)
Async XLA Ops:
  6.5 376.4 %copy-start = (bf16[256,128]{1,0:T(8,128)(2,1)S(1)}, bf16[256,128]{1,0:T(8,128)(2,1)}, u32[]{:S(2)}) copy-start(bf16[256,128]{1,0:T(8,128)(2,1)} %param.15) | copy-start | bytes 196612
  277.1 30.6 %all-to-all-start = ((s32[16,1,192]{2,1,0:T(1,128)}), s32[16,1,192]{2,1,0:T(1,128)S(1)}, u32[]{:S(2)}, u32[]{:S(2)}) async-start(s32[16,1,192]{2,1,0:T(1,128)} %all_to_all.17), calls=%async_computation | async-start | bytes 32768 | tf_op jit(solution)/shard_map/all_to_all | solution.py:89
  283.2 360.2 %all-gather.3.cloned.1.call-start = ((), (), s32[]{:S(2)}) async-start(), calls=%async_computation.4 | async-start | bytes 28311552 | tf_op jit(solution)/shard_map/all_gather | solution.py:91
  381.4 0.8 copy-start.4
  381.4 0.9 copy-start.5
  381.4 1.5 copy-start.7
  381.5 262.0 %copy-start.2 = (bf16[256,128]{1,0:T(8,128)(2,1)S(1)}, bf16[256,128]{1,0:T(8,128)(2,1)}, u32[]{:S(2)}) copy-start(bf16[256,128]{1,0:T(8,128)(2,1)} %param.16) | copy-start | bytes 196612
  381.5 262.0 %copy-start.3 = (bf16[256,128]{1,0:T(8,128)(2,1)S(1)}, bf16[256,128]{1,0:T(8,128)(2,1)}, u32[]{:S(2)}) copy-start(bf16[256,128]{1,0:T(8,128)(2,1)} %param.17) | copy-start | bytes 196612
  381.5 262.0 %copy-start.6 = (f32[128]{0:T(128)S(1)}, f32[128]{0:T(128)}, u32[]{:S(2)}) copy-start(f32[128]{0:T(128)} %param.19) | copy-start | bytes 1540
  949.4 13.1 %copy-start.1 = (bf16[256,128]{1,0:T(8,128)(2,1)S(1)}, bf16[256,128]{1,0:T(8,128)(2,1)}, u32[]{:S(2)}) copy-start(bf16[256,128]{1,0:T(8,128)(2,1)} %param.15) | copy-start | bytes 196612
Sparse Core Ops, SparseCore 0:
  381.6 261.7 all-gather.2
where the time goes:
time: 972 us; the launch traced here: 969 us
  local copies, waits for them, and re-layouts  336 us (35%)
  other arithmetic  261 us (27%)
  waiting for transfers between devices  260 us (27%)
  blocking collectives  62.7 us (6%)
  matrix products  17.4 us (2%)
  between operations  13.6 us (1%)
  loops' own time  13.2 us (1%)
    all_gather x1, waiting for transfers between devices, shards(): fetched = lax.all_gather(gotten, 'hid', axis=1, tiled=True)  260 us
    gather x16, local copies, waits for them, and re-layouts, score_block(): rows = received[where_rows].reshape(block, 2 * width, embed)  246 us
    reduce_sum x16, other arithmetic, per_owner(): asked = jnp.sum(jnp.where(equal, offsets[None, :], 0), axis=1)  242 us
    all_to_all x2, blocking collectives, cut_exchange(): lax.all_to_all(share, axis, split_axis=0, concat_axis=0, tiled=True)  52.3 us
    reshape x1, local copies, waits for them, and re-layouts, shards(): pairs_table = child_table.reshape(half, 2 * embed)  24.5 us
  transfers between devices with their start and end apart: 2, of which 1 were waited for; matrix products, arithmetic and copies ran while one was open for 3% of the time, Pallas kernels for 0%

commit v1 on v0

v1 whole, which is shorter than its diff:
```python
import functools
import math

import jax
import jax.numpy as jnp
from jax import lax
from jax.experimental import pallas as pl
from jax.experimental.pallas import tpu as pltpu
from jax.sharding import PartitionSpec as P

F32, BF16, I32 = jnp.float32, jnp.bfloat16, jnp.int32
NT = (((1,), (1,)), ((), ()))
TN = (((0,), (0,)), ((), ()))


def iota(shape, dim):
    return lax.broadcasted_iota(I32, shape, dim)


def route(h, nbeam, share, half, ids_ref, req_ref, rank_ref, a_ref, c_ref, v0_ref, v1_ref, q_ref):
    qd, width = ids_ref.shape
    lo = ids_ref[:, :128]
    hi = ids_ref[:, 128:]
    ids = jnp.concatenate([lo, hi], axis=0)
    rows = ids.shape[0]
    owner = ids // half
    before_lane = (iota((128, 128), 0) < iota((128, 128), 1)).astype(BF16)
    ones = jnp.ones((128, 128), BF16)
    both = jnp.concatenate([before_lane, ones], axis=1)
    before_row = (iota((rows, rows), 1) < iota((rows, rows), 0)).astype(BF16)
    rank = jnp.zeros((rows, 128), F32)
    for o in range(nbeam):
        hit = owner == o
        counts = jnp.dot(hit.astype(BF16), both, preferred_element_type=F32)
        above = jnp.dot(before_row, counts[:, 128:].astype(BF16), preferred_element_type=F32)
        rank = rank + jnp.where(hit, counts[:, :128] + above, 0.0)
    rank = rank.astype(I32)
    rank = jnp.concatenate([rank[:qd], rank[qd:]], axis=1)
    rank_ref[...] = rank
    ids = ids_ref[...]
    owner = ids // half
    offset = ids - owner * half
    local = rank - h * share
    place = owner * 256 + local
    inside = (local >= 0) & (local < share)
    a_ref[...] = jnp.where(inside, place // 128, -1)
    c_ref[...] = place % 128
    v0_ref[...] = (offset % 128).astype(F32)
    v1_ref[...] = (offset // 128).astype(F32)
    q_ref[...] = iota((qd, width), 0).astype(F32)
    na = 2 * nbeam
    arow = iota((na, width), 0)
    crow = iota((128, width), 0)

    def step(r, total):
        one = pl.ds(r, 1)
        hit = arow == a_ref[one, :]
        left = jnp.concatenate([jnp.where(hit, ref[one, :], 0.0) for ref in (v0_ref, v1_ref, q_ref)], axis=0)
        right = (crow == c_ref[one, :]).astype(F32)
        return total + lax.dot_general(left.astype(BF16), right.astype(BF16), NT, preferred_element_type=F32)

    table = lax.fori_loop(0, qd, step, jnp.zeros((3 * na, 128), F32), unroll=8).astype(I32)
    offs = table[:na] + 128 * table[na : 2 * na]
    qs = table[2 * na :]
    for o in range(nbeam):
        req_ref[o, 0:2, :] = offs[2 * o : 2 * o + 2]
        req_ref[o, 2:4, :] = qs[2 * o : 2 * o + 2]


def table_copies(table_ref, buf_ref, sems):
    groups = table_ref.shape[0] // 8
    width = table_ref.shape[1]
    src = table_ref.reshape(groups, 8, width)
    dst = buf_ref.reshape(groups, 4, 2, width)
    return [pltpu.make_async_copy(src.at[:, 2 * p : 2 * p + 2, :], dst.at[:, p], sems.at[p]) for p in range(4)]


def gather(share, off_ref, buf_ref, rows_ref, first, count):
    def one(b, _):
        for k in range(share):
            rows_ref[b * share + k] = buf_ref[off_ref[first + b, k // 128, k % 128]]
        return 0

    lax.fori_loop(0, count, one, 0)


def split2(x):
    hi = x.astype(BF16)
    return hi, (x - hi.astype(F32)).astype(BF16)


def score(share, b0, nb, qd, req_ref, rows_ref, queries_ref, wq_ref, wc_ref, wx_ref, vec_ref, out_ref):
    shards = wq_ref.shape[0]
    width = queries_ref.shape[1]
    m = nb * 2 * share
    qrows = []
    dup = (iota((2 * share, share), 0) // 2 == iota((2 * share, share), 1)).astype(BF16)
    for i in range(nb):
        b = b0 + i
        qvec = jnp.concatenate([req_ref[b, 2:3, :], req_ref[b, 3:4, : share - 128]], axis=1)
        oht = (iota((qd, share), 0) == qvec).astype(F32).astype(BF16)
        qb = queries_ref[pl.ds(pl.multiple_of(b * qd, qd), qd), :]
        qrow = lax.dot_general(oht, qb, TN, preferred_element_type=F32).astype(BF16)
        qrows.append(jnp.dot(dup, qrow, preferred_element_type=F32).astype(BF16))
    qrow = jnp.concatenate(qrows, axis=0) if nb > 1 else qrows[0]
    child = rows_ref[...].reshape(m, width)
    cross = child * qrow
    acc = jnp.zeros((m, 128), F32)
    for n in range(0, shards, 2):
        pair = lambda ref: jnp.concatenate([ref[n], ref[n + 1]], axis=1)
        pre = jnp.dot(child, pair(wc_ref), preferred_element_type=F32)
        pre += jnp.dot(cross, pair(wx_ref), preferred_element_type=F32)
        pre += jnp.dot(qrow, pair(wq_ref), preferred_element_type=F32)
        for j in range(2):
            part = pre[:, 128 * j : 128 * j + 128]
            acc += jnp.maximum(part + vec_ref[n + j, 0:1, :], 0.0) * vec_ref[n + j, 1:2, :]
    total = acc.T
    total = jnp.sum(total, axis=0, keepdims=True)
    for i in range(nb):
        for t in range(2 * share // 128):
            lo = i * 2 * share + t * 128
            out_ref[b0 + i, t : t + 1, :] = total[:, lo : lo + 128]


def unpermute(h, nhid, nbeam, share, half, ids_ref, rank_ref, sall_ref, out_ref):
    qd, width = ids_ref.shape
    per = width // nhid

    def own(x):
        mine = jnp.zeros((qd, per), I32)
        for k in range(nhid):
            mine = jnp.where(h == k, x[:, k * per : (k + 1) * per], mine)
        return jnp.concatenate([mine[8 * g : 8 * g + 8] for g in range(qd // 8)], axis=1)

    owner = own(ids_ref[...]) // half
    rank = own(rank_ref[...])
    chunk = rank // share
    local = rank - chunk * share
    tiles = 2 * share // 128
    row = (chunk * nbeam + owner) * tiles + local // 64
    lane = (local % 64) * 2
    nrows = nhid * nbeam * tiles
    scores = sall_ref[...].reshape(nrows, 128).T
    hi, lo = split2(scores)
    parts = jnp.concatenate([hi, lo], axis=0)
    lanes = lane.shape[1]
    rio = iota((nrows, lanes), 0)
    cio = iota((128, lanes), 0)
    evens, odds = [], []
    for i in range(8):
        onehot = (rio == row[i : i + 1]).astype(F32).astype(BF16)
        got = jnp.dot(parts, onehot, preferred_element_type=F32)
        got = got[:128] + got[128:]
        evens.append(jnp.sum(jnp.where(cio == lane[i : i + 1], got, 0.0), axis=0, keepdims=True))
        odds.append(jnp.sum(jnp.where(cio == lane[i : i + 1] + 1, got, 0.0), axis=0, keepdims=True))
    even = jnp.concatenate(split2(jnp.concatenate(evens, axis=0)), axis=0)
    odd = jnp.concatenate(split2(jnp.concatenate(odds, axis=0)), axis=0)
    n = iota((lanes, 2 * lanes), 1)
    k = iota((lanes, 2 * lanes), 0)
    mixed = jnp.dot(even, (n == 2 * k).astype(BF16), preferred_element_type=F32)
    mixed += jnp.dot(odd, (n == 2 * k + 1).astype(BF16), preferred_element_type=F32)
    mixed = mixed[:8] + mixed[8:]
    for g in range(qd // 8):
        out_ref[8 * g : 8 * g + 8, :] = mixed[:, 2 * per * g : 2 * per * (g + 1)]


BEAM, HID = 16, 8
MESH = pl.DeviceIdType.MESH


def peer_beam(b, j):
    return lax.rem(b + j, BEAM)


def peer_hid(h, j):
    return lax.rem(h + j, HID)


def entry_barrier(b, h):
    barrier = pltpu.get_barrier_semaphore()

    def beam(j, _):
        pl.semaphore_signal(barrier, inc=1, device_id=(peer_beam(b, j), h), device_id_type=MESH)
        return 0

    def hid(j, _):
        pl.semaphore_signal(barrier, inc=1, device_id=(b, peer_hid(h, j)), device_id_type=MESH)
        return 0

    lax.fori_loop(1, BEAM, beam, 0)
    lax.fori_loop(1, HID, hid, 0)
    pl.semaphore_wait(barrier, BEAM + HID - 2)


def remote(src, dst, send, recv, device):
    return pltpu.make_async_remote_copy(
        src_ref=src, dst_ref=dst, send_sem=send, recv_sem=recv, device_id=device, device_id_type=MESH
    )


def exchange_kernel(req, queries, wq, wc, wx, vec, req_all, q_all, wq_all, wc_all, wx_all, vec_all, bsend, brecv, hsend, hrecv):
    b, h = lax.axis_index("beam"), lax.axis_index("hid")
    qd = queries.shape[0]
    entry_barrier(b, h)
    spread = ((wq, wq_all), (wc, wc_all), (wx, wx_all), (vec, vec_all))

    def rows(i):
        return pl.ds(pl.multiple_of(i * qd, qd), qd)

    def beam_copies(to, sem, slot):
        device = (to, h)
        return (
            remote(req.at[to], req_all.at[slot], bsend.at[0, sem], brecv.at[0, slot], device),
            remote(queries, q_all.at[rows(slot)], bsend.at[1, sem], brecv.at[1, slot], device),
        )

    def hid_copies(to, sem, slot):
        return [
            remote(src, dst.at[slot], hsend.at[i, sem], hrecv.at[i, slot], (b, to))
            for i, (src, dst) in enumerate(spread)
        ]

    def start_hid(j, _):
        for copy in hid_copies(peer_hid(h, j), peer_hid(h, j), h):
            copy.start()
        return 0

    def start_beam(j, _):
        for copy in beam_copies(peer_beam(b, j), peer_beam(b, j), b):
            copy.start()
        return 0

    lax.fori_loop(1, BEAM, start_beam, 0)
    lax.fori_loop(1, HID, start_hid, 0)
    req_all[pl.ds(b, 1)] = req[pl.ds(b, 1)]
    q_all[rows(b), :] = queries[...]
    for src, dst in spread:
        dst[h] = src[...]

    def wait_beam(j, _):
        peer = peer_beam(b, j)
        for copy in beam_copies(peer, peer, peer):
            copy.wait()
        return 0

    def wait_hid(j, _):
        peer = peer_hid(h, j)
        for copy in hid_copies(peer, peer, peer):
            copy.wait()
        return 0

    lax.fori_loop(1, BEAM, wait_beam, 0)
    lax.fori_loop(1, HID, wait_hid, 0)


def return_kernel(scores, sall, bsend, brecv, hsend, hrecv):
    b, h = lax.axis_index("beam"), lax.axis_index("hid")
    entry_barrier(b, h)

    def back(to, slot):
        return remote(scores.at[to], sall.at[h, slot], bsend.at[to], brecv.at[slot], (to, h))

    def spread(to, slot):
        return remote(sall.at[slot], sall.at[slot], hsend.at[to], hrecv.at[slot], (b, to))

    def start_back(j, _):
        back(peer_beam(b, j), b).start()
        return 0

    def wait_back(j, _):
        back(peer_beam(b, j), peer_beam(b, j)).wait()
        return 0

    def start_spread(j, _):
        spread(peer_hid(h, j), h).start()
        return 0

    def wait_spread(j, _):
        spread(peer_hid(h, j), peer_hid(h, j)).wait()
        return 0

    lax.fori_loop(1, BEAM, start_back, 0)
    sall[h, pl.ds(b, 1)] = scores[pl.ds(b, 1)]
    lax.fori_loop(1, BEAM, wait_back, 0)
    lax.fori_loop(1, HID, start_spread, 0)
    lax.fori_loop(1, HID, wait_spread, 0)


VM = pl.BlockSpec(memory_space=pltpu.VMEM)
SM = pl.BlockSpec(memory_space=pltpu.SMEM)
ANY = pl.BlockSpec(memory_space=pl.ANY)


def shape(dims, dtype):
    return jax.ShapeDtypeStruct(dims, dtype)


def dma(*dims):
    return pltpu.SemaphoreType.DMA(dims)


def shards(queries, beam_ids, child_table, w_query, w_child, w_cross, bias, w_out):
    qd, width = beam_ids.shape
    embed = queries.shape[1]
    half = child_table.shape[0] // 2
    hid_dev = w_query.shape[1]
    share = 3 * qd * width // (2 * BEAM * HID)
    nb = 2

    def route_kernel(ids, req, rank, *scratch):
        route(lax.axis_index("hid"), BEAM, share, half, ids, req, rank, *scratch)

    req, rank = pl.pallas_call(
        route_kernel,
        out_shape=(shape((BEAM, 4, 128), I32), shape((qd, width), I32)),
        in_specs=[VM],
        out_specs=(VM, VM),
        scratch_shapes=[pltpu.VMEM((qd, width), I32)] * 2 + [pltpu.VMEM((qd, width), F32)] * 3,
        name="route",
    )(beam_ids)

    vec = jnp.stack([bias, w_out])
    req_all, q_all, wq_all, wc_all, wx_all, vec_all = pl.pallas_call(
        exchange_kernel,
        out_shape=(
            shape((BEAM, 4, 128), I32),
            shape((BEAM * qd, embed), BF16),
            *[shape((HID, embed, hid_dev), BF16)] * 3,
            shape((HID, 2, hid_dev), F32),
        ),
        in_specs=[VM] * 6,
        out_specs=(VM,) * 6,
        scratch_shapes=[dma(2, BEAM), dma(2, BEAM), dma(4, HID), dma(4, HID)],
        compiler_params=pltpu.CompilerParams(collective_id=0, has_side_effects=True),
        name="exchange",
    )(req, queries, w_query, w_child, w_cross, vec)

    def score_kernel(req, off, table, queries, wq, wc, wx, vec, out, buf, rows, sems):
        copies = table_copies(table, buf, sems)
        for copy in copies:
            copy.start()
        for copy in copies:
            copy.wait()

        def step(i, _):
            gather(share, off, buf, rows, i * nb, nb)
            score(share, i * nb, nb, qd, req, rows, queries, wq, wc, wx, vec, out)
            return 0

        lax.fori_loop(0, BEAM // nb, step, 0)

    scores = pl.pallas_call(
        score_kernel,
        out_shape=shape((BEAM, 3, 128), F32),
        in_specs=[VM, SM, ANY, VM, VM, VM, VM, VM],
        out_specs=VM,
        scratch_shapes=[
            pltpu.VMEM((half, 2, embed), BF16),
            pltpu.VMEM((nb * share, 2, embed), BF16),
            dma(4),
        ],
        compiler_params=pltpu.CompilerParams(vmem_limit_bytes=56 * 2**20),
        name="score",
    )(req_all, req_all, child_table, q_all, wq_all, wc_all, wx_all, vec_all)

    sall = pl.pallas_call(
        return_kernel,
        out_shape=shape((HID, BEAM, 3, 128), F32),
        in_specs=[VM],
        out_specs=VM,
        scratch_shapes=[dma(BEAM), dma(BEAM), dma(HID), dma(HID)],
        compiler_params=pltpu.CompilerParams(collective_id=1, has_side_effects=True),
        name="give_back",
    )(scores)

    def place_kernel(ids, rank, sall, out):
        unpermute(lax.axis_index("hid"), HID, BEAM, share, half, ids, rank, sall, out)

    return pl.pallas_call(
        place_kernel,
        out_shape=shape((qd, 2 * width // HID), F32),
        in_specs=[VM] * 3,
        out_specs=VM,
        name="place",
    )(beam_ids, rank, sall)


def solution(mesh):
    return jax.shard_map(
        shards,
        mesh=mesh,
        in_specs=(
            P("beam", None),
            P("beam", None),
            P("beam", None),
            P(None, "hid"),
            P(None, "hid"),
            P(None, "hid"),
            P("hid"),
            P("hid"),
        ),
        out_specs=P("beam", "hid"),
        check_vma=False,
    )
```

time: 972 us -> 94.4 us (0.10)
  local copies, waits for them, and re-layouts: 336 us -> 0 us
  waiting for transfers between devices: 260 us -> 0 us
  other arithmetic: 261 us -> 1.26 us
  Pallas kernels: 0 us -> 92.8 us
  blocking collectives: 62.7 us -> 0 us
  matrix products: 17.4 us -> 0 us
  between operations: 13.6 us -> 0.03 us
  loops' own time: 13.2 us -> 0 us
    gather x17 -> x0, local copies, waits for them, and re-layouts: 265 us -> none  [the longest x16 246 us: score_block(): rows = received[where_rows].reshape(block, 2 * width, embed)]
    all_gather x1 -> x0, waiting for transfers between devices: 260 us -> none  [shards(): fetched = lax.all_gather(gotten, 'hid', axis=1, tiled=True)]
    reduce_sum x18 -> x0, other arithmetic: 243 us -> none  [the longest x16 242 us: per_owner(): asked = jnp.sum(jnp.where(equal, offsets[None, :], 0), axis=1)]
    pallas_call x0 -> x5, Pallas kernels: none -> 92.8 us  [the longest x1 37.9 us: shards(): pl.pallas_call(exchange_kernel, out_shape=(shape((BEAM, 4, 128), I32), sh...]
    all_to_all x3 -> x0, blocking collectives: 62.7 us -> none  [the longest x2 52.3 us: cut_exchange(): lax.all_to_all(share, axis, split_axis=0, concat_axis=0, tiled=True)]
    reshape x20 -> x0, local copies, waits for them, and re-layouts: 32.3 us -> none  [the longest x1 24.5 us: shards(): pairs_table = child_table.reshape(half, 2 * embed)]
    dynamic_slice x49 -> x0, local copies, waits for them, and re-layouts: 23.2 us -> none  [the longest x32 12.5 us: shards(): lax.map(score_block, (position.reshape(blocks, block * width), queries.re...]
    dot_general x34 -> x0, matrix products: 17.4 us -> none  [the longest x16 8.36 us: score_block(): jnp.dot(flat_cross, w_cross, preferred_element_type=jnp.float32)]
  transfers between devices with their start and end apart: 2 -> 0, of which waited for: 1 -> 0; matrix products, arithmetic and copies ran while one was open for 3% -> 0% of each run, Pallas kernels for 0% -> 0%
where the time goes in v1:
time: 94.4 us; the launch traced here: 94.1 us
  Pallas kernels  92.8 us (98%)
  other arithmetic  1.26 us (1%)
    pallas_call x1, Pallas kernels, shards(): pl.pallas_call(exchange_kernel, out_shape=(shape((BEAM, 4, 128), I32), sh...  37.9 us
    pallas_call x1, Pallas kernels, shards(): pl.pallas_call(score_kernel, out_shape=shape((BEAM, 3, 128), F32), in_spe...  26.4 us
    pallas_call x1, Pallas kernels, shards(): pl.pallas_call(return_kernel, out_shape=shape((HID, BEAM, 3, 128), F32),...  18.1 us
    pallas_call x1, Pallas kernels, shards(): pl.pallas_call(route_kernel, out_shape=(shape((BEAM, 4, 128), I32), shape...  6.83 us
    pallas_call x1, Pallas kernels, shards(): pl.pallas_call(place_kernel, out_shape=shape((qd, 2 * width // HID), F32)...  3.53 us

profile of v1, /device:TPU:0, one launch (start us, length us, event | category | flops | bytes accessed | tf_op | source)
XLA Modules:
  0.0 94.1 jit_solution(10298185125533721996)
XLA Ops:
  0.0 1.3 %pad_maximum_fusion.vec = f32[2,128]{1,0:T(2,128)} fusion(f32[1,128]{1,0:T(1,128)} %bitcast.2, f32[1,128]{1,0:T(1,128)} %bitcast.3), kind=kLoop, calls=%fused_computation | loop fusion | flops 256 | bytes 2048 | tf_op jit(solution)/shard_map/stack | solution.py:322
  1.3 6.8 %route.1 = (s32[16,4,128]{2,1,0:T(4,128)}, s32[64,256]{1,0:T(8,128)}) custom-call(s32[64,256]{1,0:T(8,128)} %ids.3), custom_call_target="tpu_custom_call" | custom-call | tf_op jit(solution)/shard_map/route/pallas_call | solution.py:313
  8.1 37.9 %exchange.1 = (s32[16,4,128]{2,1,0:T(4,128)}, bf16[1024,256]{1,0:T(8,128)(2,1)}, bf16[8,256,128]{2,1,0:T(8,128)(2,1)}, bf16[8,256,128]{2,1,0:T(8,128)(2,1)}, bf1...) custom-call(s32[16,4,128]{2,1,0:T(4,128)} %get-tuple-element.14.req, bf16[64,256]{1,0:T(8,128)(2,1)} %queries.1, ...), custom_call_target="tpu_custom_call" | custom-call | tf_op jit(solution)/shard_map/exchange/pallas_call | solution.py:323
  46.0 26.4 %score.1.scores = f32[16,3,128]{2,1,0:T(4,128)} custom-call(s32[16,4,128]{2,1,0:T(4,128)} %get-tuple-element.15.req.off, s32[16,4,128]{2,1,0:T(4,128)} %get-tuple-element.15.req.off, bf16[32768,256]{1,0:T(8,128)(2,1)} %table.1, bf16[1024,256]{1,0:T(8,128)(2,1)} %get-tuple-element.16.queries, bf16[8,256,128]{2,1,0:T(8,128)(2,1)} %get-tuple-element.17.wq, ...), custom_call_target="tpu_custom_call" | custom-call | tf_op jit(solution)/shard_map/score/pallas_call | solution.py:352
  72.5 18.1 %give_back.1.sall = f32[8,16,3,128]{3,2,1,0:T(4,128)} custom-call(f32[16,3,128]{2,1,0:T(4,128)} %score.1.scores), custom_call_target="tpu_custom_call" | custom-call | tf_op jit(solution)/shard_map/give_back/pallas_call | solution.py:366
  90.5 3.5 %place.1 = f32[64,64]{1,0:T(8,128)} custom-call(s32[64,256]{1,0:T(8,128)} %ids.3, s32[64,256]{1,0:T(8,128)} %get-tuple-element.13.rank, f32[8,16,3,128]{3,2,1,0:T(4,128)} %give_back.1.sall), custom_call_target="tpu_custom_call" | custom-call | tf_op jit(solution)/shard_map/place/pallas_call | solution.py:379

commit v2 on v1

--- a/solution.py
+++ b/solution.py
@@ -166,30 +166,16 @@
 
 BEAM, HID = 16, 8
 MESH = pl.DeviceIdType.MESH
-
-
-def peer_beam(b, j):
-    return lax.rem(b + j, BEAM)
-
-
-def peer_hid(h, j):
-    return lax.rem(h + j, HID)
-
-
-def entry_barrier(b, h):
-    barrier = pltpu.get_barrier_semaphore()
-
-    def beam(j, _):
-        pl.semaphore_signal(barrier, inc=1, device_id=(peer_beam(b, j), h), device_id_type=MESH)
-        return 0
-
-    def hid(j, _):
-        pl.semaphore_signal(barrier, inc=1, device_id=(b, peer_hid(h, j)), device_id_type=MESH)
-        return 0
-
-    lax.fori_loop(1, BEAM, beam, 0)
-    lax.fori_loop(1, HID, hid, 0)
-    pl.semaphore_wait(barrier, BEAM + HID - 2)
+VM = pl.BlockSpec(memory_space=pltpu.VMEM)
+ANY = pl.BlockSpec(memory_space=pl.ANY)
+
+
+def shape(dims, dtype):
+    return jax.ShapeDtypeStruct(dims, dtype)
+
+
+def dma(*dims):
+    return pltpu.SemaphoreType.DMA(dims)
 
 
 def remote(src, dst, send, recv, device):
@@ -198,64 +184,162 @@
     )
 
 
-def exchange_kernel(req, queries, wq, wc, wx, vec, req_all, q_all, wq_all, wc_all, wx_all, vec_all, bsend, brecv, hsend, hrecv):
+def loop(lo, hi, body):
+    def step(i, _):
+        body(i)
+        return 0
+
+    lax.fori_loop(lo, hi, step, 0)
+
+
+def front_kernel(
+    share,
+    ids,
+    queries,
+    wq,
+    wc,
+    wx,
+    bias,
+    w_out,
+    table,
+    rank,
+    req_all,
+    q_all,
+    w_all,
+    vec_all,
+    buf,
+    req,
+    a_ref,
+    c_ref,
+    v0_ref,
+    v1_ref,
+    qi_ref,
+    table_sem,
+    own_sem,
+    rsend,
+    rrecv,
+    qsend,
+    qrecv,
+    vsend,
+    vrecv,
+    wsend,
+    wrecv,
+    psend,
+    precv,
+):
     b, h = lax.axis_index("beam"), lax.axis_index("hid")
-    qd = queries.shape[0]
-    entry_barrier(b, h)
-    spread = ((wq, wq_all), (wc, wc_all), (wx, wx_all), (vec, vec_all))
-
-    def rows(i):
+    core = lax.rem(b, 2)
+    mate = b + 1 - 2 * core
+    z = lax.rem(h, 2)
+    across = h + 1 - 2 * z
+    qd = ids.shape[0]
+    half = table.shape[0] // 2
+    depth = w_all.shape[2] // 2
+
+    def beam_peer(j):
+        return lax.rem(b + j, BEAM)
+
+    def hid_peer(j):
+        return lax.rem(h + j, HID)
+
+    def x_peer(j):
+        return lax.rem(h + 2 * j, HID)
+
+    barrier = pltpu.get_barrier_semaphore()
+    loop(1, BEAM, lambda j: pl.semaphore_signal(barrier, inc=1, device_id=(beam_peer(j), h), device_id_type=MESH))
+    loop(1, HID, lambda j: pl.semaphore_signal(barrier, inc=1, device_id=(b, hid_peer(j)), device_id_type=MESH))
+
+    def q_rows(i):
         return pl.ds(pl.multiple_of(i * qd, qd), qd)
 
-    def beam_copies(to, sem, slot):
-        device = (to, h)
-        return (
-            remote(req.at[to], req_all.at[slot], bsend.at[0, sem], brecv.at[0, slot], device),
-            remote(queries, q_all.at[rows(slot)], bsend.at[1, sem], brecv.at[1, slot], device),
-        )
-
-    def hid_copies(to, sem, slot):
-        return [
-            remote(src, dst.at[slot], hsend.at[i, sem], hrecv.at[i, slot], (b, to))
-            for i, (src, dst) in enumerate(spread)
-        ]
-
-    def start_hid(j, _):
-        for copy in hid_copies(peer_hid(h, j), peer_hid(h, j), h):
-            copy.start()
-        return 0
-
-    def start_beam(j, _):
-        for copy in beam_copies(peer_beam(b, j), peer_beam(b, j), b):
-            copy.start()
-        return 0
-
-    lax.fori_loop(1, BEAM, start_beam, 0)
-    lax.fori_loop(1, HID, start_hid, 0)
+    own = [
+        pltpu.make_async_copy(src, w_all.at[h, i], own_sem.at[i]) for i, src in enumerate((wq, wc, wx))
+    ]
+    own.append(pltpu.make_async_copy(queries, q_all.at[q_rows(b), :], own_sem.at[3]))
+    own.append(pltpu.make_async_copy(bias, vec_all.at[h, 0:1, :], own_sem.at[4]))
+    own.append(pltpu.make_async_copy(w_out, vec_all.at[h, 1:2, :], own_sem.at[5]))
+    for copy in own:
+        copy.start()
+    pulls = table_copies(table, buf, table_sem)
+    for copy in pulls:
+        copy.start()
+    for copy in own:
+        copy.wait()
+    pl.semaphore_wait(barrier, BEAM + HID - 2)
+
+    def piece(shard, part):
+        return w_all.at[shard, :, pl.ds(pl.multiple_of(part * depth, depth), depth), :]
+
+    def w_copy(shard, to, slot):
+        return remote(piece(shard, core), piece(shard, core), wsend.at[slot], wrecv.at[shard], (b, to))
+
+    def mate_copy(shard):
+        return remote(piece(shard, core), piece(shard, core), psend.at[shard], precv.at[shard], (mate, h))
+
+    def mate_arrival(shard):
+        other = piece(shard, 1 - core)
+        return remote(other, other, psend.at[shard], precv.at[shard], (mate, h))
+
+    def q_copy(to, slot):
+        return remote(q_all.at[q_rows(slot), :], q_all.at[q_rows(slot), :], qsend.at[to], qrecv.at[slot], (to, h))
+
+    def v_copy(to, slot):
+        return remote(vec_all.at[slot], vec_all.at[slot], vsend.at[to], vrecv.at[slot], (b, to))
+
+    def r_copy(to, slot):
+        return remote(req.at[to], req_all.at[slot], rsend.at[to], rrecv.at[slot], (to, h))
+
+    w_copy(h, across, 0).start()
+    for j in range(1, 4):
+        w_copy(h, x_peer(j), j).start()
+    loop(1, HID, lambda j: v_copy(hid_peer(j), h).start())
+    loop(1, BEAM, lambda j: q_copy(beam_peer(j), b).start())
+
+    route(h, BEAM, share, half, ids, req, rank, a_ref, c_ref, v0_ref, v1_ref, qi_ref)
+    loop(1, BEAM, lambda j: r_copy(beam_peer(j), b).start())
     req_all[pl.ds(b, 1)] = req[pl.ds(b, 1)]
-    q_all[rows(b), :] = queries[...]
-    for src, dst in spread:
-        dst[h] = src[...]
-
-    def wait_beam(j, _):
-        peer = peer_beam(b, j)
-        for copy in beam_copies(peer, peer, peer):
-            copy.wait()
-        return 0
-
-    def wait_hid(j, _):
-        peer = peer_hid(h, j)
-        for copy in hid_copies(peer, peer, peer):
-            copy.wait()
-        return 0
-
-    lax.fori_loop(1, BEAM, wait_beam, 0)
-    lax.fori_loop(1, HID, wait_hid, 0)
-
-
-def return_kernel(scores, sall, bsend, brecv, hsend, hrecv):
+
+    w_copy(across, across, 0).wait_recv()
+    for j in range(1, 4):
+        w_copy(across, x_peer(j), 3 + j).start()
+    mate_copy(across).start()
+
+    loop(1, BEAM, lambda j: r_copy(beam_peer(j), beam_peer(j)).wait_recv())
+    for copy in pulls:
+        copy.wait()
+
+    for j in range(1, 4):
+        for zz in (h, across):
+            shard = lax.rem(zz + 2 * j, HID)
+            w_copy(shard, shard, 0).wait_recv()
+            mate_copy(shard).start()
+    loop(1, BEAM, lambda j: q_copy(beam_peer(j), beam_peer(j)).wait_recv())
+    loop(1, HID, lambda j: v_copy(hid_peer(j), hid_peer(j)).wait_recv())
+    loop(1, HID, lambda j: mate_arrival(hid_peer(j)).wait_recv())
+
+    w_copy(h, across, 0).wait_send()
+    for j in range(1, 4):
+        w_copy(h, x_peer(j), j).wait_send()
+        w_copy(across, x_peer(j), 3 + j).wait_send()
+    loop(1, BEAM, lambda j: q_copy(beam_peer(j), b).wait_send())
+    loop(1, BEAM, lambda j: r_copy(beam_peer(j), b).wait_send())
+    loop(1, HID, lambda j: v_copy(hid_peer(j), h).wait_send())
+    loop(1, HID, lambda j: mate_copy(hid_peer(j)).wait_send())
+
+
+def back_kernel(scores, sall, bsend, brecv, hsend, hrecv):
     b, h = lax.axis_index("beam"), lax.axis_index("hid")
-    entry_barrier(b, h)
+
+    def beam_peer(j):
+        return lax.rem(b + j, BEAM)
+
+    def hid_peer(j):
+        return lax.rem(h + j, HID)
+
+    barrier = pltpu.get_barrier_semaphore()
+    loop(1, BEAM, lambda j: pl.semaphore_signal(barrier, inc=1, device_id=(beam_peer(j), h), device_id_type=MESH))
+    loop(1, HID, lambda j: pl.semaphore_signal(barrier, inc=1, device_id=(b, hid_peer(j)), device_id_type=MESH))
+    pl.semaphore_wait(barrier, BEAM + HID - 2)
 
     def back(to, slot):
         return remote(scores.at[to], sall.at[h, slot], bsend.at[to], brecv.at[slot], (to, h))
@@ -263,40 +347,21 @@
     def spread(to, slot):
         return remote(sall.at[slot], sall.at[slot], hsend.at[to], hrecv.at[slot], (b, to))
 
-    def start_back(j, _):
-        back(peer_beam(b, j), b).start()
-        return 0
-
-    def wait_back(j, _):
-        back(peer_beam(b, j), peer_beam(b, j)).wait()
-        return 0
-
-    def start_spread(j, _):
-        spread(peer_hid(h, j), h).start()
-        return 0
-
-    def wait_spread(j, _):
-        spread(peer_hid(h, j), peer_hid(h, j)).wait()
-        return 0
-
-    lax.fori_loop(1, BEAM, start_back, 0)
+    loop(1, BEAM, lambda j: back(beam_peer(j), b).start())
     sall[h, pl.ds(b, 1)] = scores[pl.ds(b, 1)]
-    lax.fori_loop(1, BEAM, wait_back, 0)
-    lax.fori_loop(1, HID, start_spread, 0)
-    lax.fori_loop(1, HID, wait_spread, 0)
-
-
-VM = pl.BlockSpec(memory_space=pltpu.VMEM)
-SM = pl.BlockSpec(memory_space=pltpu.SMEM)
-ANY = pl.BlockSpec(memory_space=pl.ANY)
-
-
-def shape(dims, dtype):
-    return jax.ShapeDtypeStruct(dims, dtype)
-
-
-def dma(*dims):
-    return pltpu.SemaphoreType.DMA(dims)
+    loop(1, BEAM, lambda j: back(beam_peer(j), beam_peer(j)).wait_recv())
+    loop(1, HID, lambda j: spread(hid_peer(j), h).start())
+    loop(1, BEAM, lambda j: back(beam_peer(j), b).wait_send())
+    loop(1, HID, lambda j: spread(hid_peer(j), h).wait_send())
+    loop(1, HID, lambda j: spread(hid_peer(j), hid_peer(j)).wait_recv())
+
+
+def score_kernel(share, nb, qd, req, off, queries, w_all, vec, buf, scores, rows):
+    def step(i):
+        gather(share, off, buf, rows, i * nb, nb)
+        score(share, i * nb, nb, qd, req, rows, queries, w_all.at[:, 0], w_all.at[:, 1], w_all.at[:, 2], vec, scores)
+
+    loop(0, BEAM // nb, step)
 
 
 def shards(queries, beam_ids, child_table, w_query, w_child, w_cross, bias, w_out):
@@ -305,66 +370,53 @@
     half = child_table.shape[0] // 2
     hid_dev = w_query.shape[1]
     share = 3 * qd * width // (2 * BEAM * HID)
-    nb = 2
-
-    def route_kernel(ids, req, rank, *scratch):
-        route(lax.axis_index("hid"), BEAM, share, half, ids, req, rank, *scratch)
-
-    req, rank = pl.pallas_call(
-        route_kernel,
-        out_shape=(shape((BEAM, 4, 128), I32), shape((qd, width), I32)),
-        in_specs=[VM],
-        out_specs=(VM, VM),
-        scratch_shapes=[pltpu.VMEM((qd, width), I32)] * 2 + [pltpu.VMEM((qd, width), F32)] * 3,
-        name="route",
-    )(beam_ids)
-
-    vec = jnp.stack([bias, w_out])
-    req_all, q_all, wq_all, wc_all, wx_all, vec_all = pl.pallas_call(
-        exchange_kernel,
+    nb = 4
+    ints = pltpu.VMEM((qd, width), I32)
+    floats = pltpu.VMEM((qd, width), F32)
+
+    rank, req_all, q_all, w_all, vec_all, buf = pl.pallas_call(
+        functools.partial(front_kernel, share),
         out_shape=(
+            shape((qd, width), I32),
             shape((BEAM, 4, 128), I32),
-            shape((BEAM * qd, embed), BF16),
-            *[shape((HID, embed, hid_dev), BF16)] * 3,
-            shape((HID, 2, hid_dev), F32),
+            pltpu.VMEM((BEAM * qd, embed), BF16),
+            pltpu.VMEM((HID, 3, embed, hid_dev), BF16),
+            pltpu.VMEM((HID, 2, hid_dev), F32),
+            pltpu.VMEM((half, 2, embed), BF16),
         ),
-        in_specs=[VM] * 6,
+        in_specs=[VM] + [ANY] * 7,
         out_specs=(VM,) * 6,
-        scratch_shapes=[dma(2, BEAM), dma(2, BEAM), dma(4, HID), dma(4, HID)],
-        compiler_params=pltpu.CompilerParams(collective_id=0, has_side_effects=True),
-        name="exchange",
-    )(req, queries, w_query, w_child, w_cross, vec)
-
-    def score_kernel(req, off, table, queries, wq, wc, wx, vec, out, buf, rows, sems):
-        copies = table_copies(table, buf, sems)
-        for copy in copies:
-            copy.start()
-        for copy in copies:
-            copy.wait()
-
-        def step(i, _):
-            gather(share, off, buf, rows, i * nb, nb)
-            score(share, i * nb, nb, qd, req, rows, queries, wq, wc, wx, vec, out)
-            return 0
-
-        lax.fori_loop(0, BEAM // nb, step, 0)
+        scratch_shapes=[
+            pltpu.VMEM((BEAM, 4, 128), I32),
+            ints,
+            ints,
+            floats,
+            floats,
+            floats,
+            dma(4),
+            dma(6),
+            *[dma(BEAM)] * 4,
+            *[dma(HID)] * 2,
+            dma(7),
+            dma(HID),
+            *[dma(HID)] * 2,
+        ],
+        compiler_params=pltpu.CompilerParams(collective_id=0, has_side_effects=True, vmem_limit_bytes=6 * 2**20),
+        name="front",
+    )(beam_ids, queries, w_query, w_child, w_cross, bias.reshape(1, -1), w_out.reshape(1, -1), child_table)
 
     scores = pl.pallas_call(
-        score_kernel,
+        functools.partial(score_kernel, share, nb, qd),
         out_shape=shape((BEAM, 3, 128), F32),
-        in_specs=[VM, SM, ANY, VM, VM, VM, VM, VM],
+        in_specs=[VM, pl.BlockSpec(memory_space=pltpu.SMEM)] + [VM] * 4,
         out_specs=VM,
-        scratch_shapes=[
-            pltpu.VMEM((half, 2, embed), BF16),
-            pltpu.VMEM((nb * share, 2, embed), BF16),
-            dma(4),
-        ],
-        compiler_params=pltpu.CompilerParams(vmem_limit_bytes=56 * 2**20),
+        scratch_shapes=[pltpu.VMEM((nb * share, 2, embed), BF16)],
+        compiler_params=pltpu.CompilerParams(vmem_limit_bytes=20 * 2**20),
         name="score",
-    )(req_all, req_all, child_table, q_all, wq_all, wc_all, wx_all, vec_all)
+    )(req_all, req_all, q_all, w_all, vec_all, buf)
 
     sall = pl.pallas_call(
-        return_kernel,
+        back_kernel,
         out_shape=shape((HID, BEAM, 3, 128), F32),
         in_specs=[VM],
         out_specs=VM,

time: 94.4 us -> 84.8 us (0.90)
  Pallas kernels: 92.8 us -> 71.9 us
  local copies, waits for them, and re-layouts: 0 us -> 12.4 us
  other arithmetic: 1.26 us -> 0 us
    pallas_call x4 -> x3, Pallas kernels: 89.2 us -> 68.3 us  [the longest x1 32.8 us: shards(): pl.pallas_call(functools.partial(front_kernel, share), out_shape=(shape((...]
    unnamed x0 -> x20, local copies, waits for them, and re-layouts: none -> 12.4 us
    another operation x1 -> x0, other arithmetic: 1.26 us -> none  [shards(): vec = jnp.stack([bias, w_out])]
where the time goes in v2:
time: 84.8 us; the launch traced here: 84.3 us
  Pallas kernels  71.9 us (85%)
  local copies, waits for them, and re-layouts  12.4 us (15%)
    pallas_call x1, Pallas kernels, shards(): pl.pallas_call(functools.partial(front_kernel, share), out_shape=(shape((...  32.8 us
    pallas_call x1, Pallas kernels, shards(): pl.pallas_call(functools.partial(score_kernel, share, nb, qd), out_shape=...  18.9 us
    pallas_call x1, Pallas kernels, shards(): pl.pallas_call(back_kernel, out_shape=shape((HID, BEAM, 3, 128), F32), in...  16.7 us
    unnamed x20, local copies, waits for them, and re-layouts  12.4 us
    pallas_call x1, Pallas kernels, shards(): pl.pallas_call(place_kernel, out_shape=shape((qd, 2 * width // HID), F32)...  3.53 us

profile of v2, /device:TPU:0, one launch (start us, length us, event | category | flops | bytes accessed | tf_op | source)
XLA Modules:
  0.0 84.3 jit_solution(2203618686282349279)
XLA Ops:
  0.0 0.0 copy-start
  0.0 5.8 %copy-done = bf16[32768,256]{1,0:T(8,128)(2,1)S(1)} copy-done((bf16[32768,256]{1,0:T(8,128)(2,1)S(1)}, bf16[32768,256]{1,0:T(8,128)(2,1)}, u32[]{:S(2)}) %copy-start) | copy-done | bytes 16777240
  5.8 0.0 copy-start.1
  5.8 0.8 copy-done.1
  6.6 0.0 copy-start.3
  6.6 0.8 copy-done.3
  7.5 0.0 copy-start.4
  7.5 0.8 copy-done.4
  8.3 0.0 copy-start.5
  8.3 0.8 copy-done.5
  9.1 0.0 copy-start.7
  9.1 0.8 copy-done.7
  9.9 0.0 copy-start.8
  9.9 0.7 copy-done.8
  10.5 0.0 copy-start.9
  10.5 0.7 copy-done.9
  11.2 32.8 %front.1 = (s32[64,256]{1,0:T(8,128)S(1)}, s32[16,4,128]{2,1,0:T(4,128)S(1)}, bf16[1024,256]{1,0:T(8,128)(2,1)S(1)}, bf16[8,3,256,128]{3,2,1,0:T(8,128)(2,1)S(1)...) custom-call(s32[64,256]{1,0:T(8,128)S(1)} %copy-done.1, bf16[64,256]{1,0:T(8,128)(2,1)S(1)} %copy-done.7, ...), custom_call_target="tpu_custom_call" | custom-call | tf_op jit(solution)/shard_map/front/pallas_call | solution.py:377
  44.0 0.0 copy-start.6
  44.0 0.6 copy-done.6
  44.6 18.9 %score.1.scores = f32[16,3,128]{2,1,0:T(4,128)S(1)} custom-call(s32[16,4,128]{2,1,0:T(4,128)S(1)} %get-tuple-element.12.req.off, s32[16,4,128]{2,1,0:T(4,128)S(1)} %get-tuple-element.12.req.off, bf16[1024,256]{1,0:T(8,128)(2,1)S(1)} %get-tuple-element.13.queries, bf16[8,3,256,128]{3,2,1,0:T(8,128)(2,1)S(1)} %get-tuple-element.14.w_all, ...), custom_call_target="tpu_custom_call" | custom-call | tf_op jit(solution)/shard_map/score/pallas_call | solution.py:408
  63.5 0.0 copy-start.2
  63.5 0.6 copy-done.2
  64.1 16.7 %give_back.1.sall = f32[8,16,3,128]{3,2,1,0:T(4,128)} custom-call(f32[16,3,128]{2,1,0:T(4,128)} %copy-done.2), custom_call_target="tpu_custom_call" | custom-call | tf_op jit(solution)/shard_map/give_back/pallas_call | solution.py:418
  80.8 3.5 %place.1 = f32[64,64]{1,0:T(8,128)} custom-call(s32[64,256]{1,0:T(8,128)} %ids.3, s32[64,256]{1,0:T(8,128)} %copy-done.6, f32[8,16,3,128]{3,2,1,0:T(4,128)} %give_back.1.sall), custom_call_target="tpu_custom_call" | custom-call | tf_op jit(solution)/shard_map/place/pallas_call | solution.py:431
Async XLA Ops:
  0.0 5.8 %copy-start = (bf16[32768,256]{1,0:T(8,128)(2,1)S(1)}, bf16[32768,256]{1,0:T(8,128)(2,1)}, u32[]{:S(2)}) copy-start(bf16[32768,256]{1,0:T(8,128)(2,1)} %table.1) | copy-start | bytes 50331652
  5.8 0.8 copy-start.1
  6.6 0.8 copy-start.3
  7.5 0.8 copy-start.4
  8.3 0.8 copy-start.5
  9.1 0.8 copy-start.7
  9.9 0.7 copy-start.8
  10.5 0.7 copy-start.9
  44.0 0.6 copy-start.6
  63.5 0.6 copy-start.2

commit v3 on v2

--- a/solution.py
+++ b/solution.py
@@ -167,7 +167,7 @@
 BEAM, HID = 16, 8
 MESH = pl.DeviceIdType.MESH
 VM = pl.BlockSpec(memory_space=pltpu.VMEM)
-ANY = pl.BlockSpec(memory_space=pl.ANY)
+ANY = pl.BlockSpec(memory_space=pltpu.HBM)
 
 
 def shape(dims, dtype):
@@ -401,7 +401,7 @@
             dma(HID),
             *[dma(HID)] * 2,
         ],
-        compiler_params=pltpu.CompilerParams(collective_id=0, has_side_effects=True, vmem_limit_bytes=6 * 2**20),
+        compiler_params=pltpu.CompilerParams(collective_id=0, has_side_effects=True, vmem_limit_bytes=45 * 2**20),
         name="front",
     )(beam_ids, queries, w_query, w_child, w_cross, bias.reshape(1, -1), w_out.reshape(1, -1), child_table)
 

time: 84.8 us -> 64.5 us (0.76)
  local copies, waits for them, and re-layouts: 12.4 us -> 1.36 us
  Pallas kernels: 71.9 us -> 62.8 us
    unnamed x20 -> x4, local copies, waits for them, and re-layouts: 12.4 us -> 1.36 us
    pallas_call x1, Pallas kernels: 32.8 us -> 27.1 us  [shards(): pl.pallas_call(functools.partial(front_kernel, share), out_shape=(shape((...]
    pallas_call x1, Pallas kernels: 16.7 us -> 13.6 us  [shards(): pl.pallas_call(back_kernel, out_shape=shape((HID, BEAM, 3, 128), F32), in...]
where the time goes in v3:
time: 64.5 us; the launch traced here: 64.2 us
  Pallas kernels  62.8 us (97%)
  local copies, waits for them, and re-layouts  1.36 us (2%)
    pallas_call x1, Pallas kernels, shards(): pl.pallas_call(functools.partial(front_kernel, share), out_shape=(shape((...  27.1 us
    pallas_call x1, Pallas kernels, shards(): pl.pallas_call(functools.partial(score_kernel, share, nb, qd), out_shape=...  18.6 us
    pallas_call x1, Pallas kernels, shards(): pl.pallas_call(back_kernel, out_shape=shape((HID, BEAM, 3, 128), F32), in...  13.6 us
    pallas_call x1, Pallas kernels, shards(): pl.pallas_call(place_kernel, out_shape=shape((qd, 2 * width // HID), F32)...  3.54 us
    unnamed x4, local copies, waits for them, and re-layouts  1.36 us

profile of v3, /device:TPU:0, one launch (start us, length us, event | category | flops | bytes accessed | tf_op | source)
XLA Modules:
  0.0 64.2 jit_solution(8395515313958064097)
XLA Ops:
  0.0 27.1 %front.1 = (s32[64,256]{1,0:T(8,128)}, s32[16,4,128]{2,1,0:T(4,128)}, bf16[1024,256]{1,0:T(8,128)(2,1)S(1)}, bf16[8,3,256,128]{3,2,1,0:T(8,128)(2,1)S(1)}, f32[8...) custom-call(s32[64,256]{1,0:T(8,128)} %ids.3, bf16[64,256]{1,0:T(8,128)(2,1)} %queries.1, bf16[256,128]{1,0:T(8,128)(2,1)} %wq.1, ...), custom_call_target="tpu_custom_call" | custom-call | tf_op jit(solution)/shard_map/front/pallas_call | solution.py:377
  27.1 0.0 copy-start
  27.1 0.7 %copy-done = s32[16,4,128]{2,1,0:T(4,128)S(1)} copy-done((s32[16,4,128]{2,1,0:T(4,128)S(1)}, s32[16,4,128]{2,1,0:T(4,128)}, u32[]{:S(2)}) %copy-start) | copy-done | bytes 32792
  27.8 18.6 %score.1.scores = f32[16,3,128]{2,1,0:T(4,128)S(1)} custom-call(s32[16,4,128]{2,1,0:T(4,128)S(1)} %copy-done, s32[16,4,128]{2,1,0:T(4,128)S(1)} %copy-done, bf16[1024,256]{1,0:T(8,128)(2,1)S(1)} %get-tuple-element.13.queries, bf16[8,3,256,128]{3,2,1,0:T(8,128)(2,1)S(1)} %get-tuple-element.14.w_all, f32[8,2,128]{2,1,0:T(2,128)S(1)} %get-tuple-element.15.vec, ...), custom_call_target="tpu_custom_call" | custom-call | tf_op jit(solution)/shard_map/score/pallas_call | solution.py:408
  46.4 0.0 copy-start.1
  46.4 0.6 copy-done.1
  47.0 13.6 %give_back.1.sall = f32[8,16,3,128]{3,2,1,0:T(4,128)} custom-call(f32[16,3,128]{2,1,0:T(4,128)} %copy-done.1), custom_call_target="tpu_custom_call" | custom-call | tf_op jit(solution)/shard_map/give_back/pallas_call | solution.py:418
  60.6 3.5 %place.1 = f32[64,64]{1,0:T(8,128)} custom-call(s32[64,256]{1,0:T(8,128)} %ids.3, s32[64,256]{1,0:T(8,128)} %get-tuple-element.11.rank, f32[8,16,3,128]{3,2,1,0:T(4,128)} %give_back.1.sall), custom_call_target="tpu_custom_call" | custom-call | tf_op jit(solution)/shard_map/place/pallas_call | solution.py:431
Async XLA Ops:
  27.1 0.8 %copy-start = (s32[16,4,128]{2,1,0:T(4,128)S(1)}, s32[16,4,128]{2,1,0:T(4,128)}, u32[]{:S(2)}) copy-start(s32[16,4,128]{2,1,0:T(4,128)} %get-tuple-element.12.req.off) | copy-start | bytes 98308
  46.4 0.6 copy-start.1

commit v4 on v3

--- a/solution.py
+++ b/solution.py
@@ -17,7 +17,7 @@
     return lax.broadcasted_iota(I32, shape, dim)
 
 
-def route(h, nbeam, share, half, ids_ref, req_ref, rank_ref, a_ref, c_ref, v0_ref, v1_ref, q_ref):
+def route(h, nbeam, share, half, midway, ids_ref, req_ref, rank_ref, a_ref, c_ref, v0_ref, v1_ref, q_ref):
     qd, width = ids_ref.shape
     lo = ids_ref[:, :128]
     hi = ids_ref[:, 128:]
@@ -59,7 +59,9 @@
         right = (crow == c_ref[one, :]).astype(F32)
         return total + lax.dot_general(left.astype(BF16), right.astype(BF16), NT, preferred_element_type=F32)
 
-    table = lax.fori_loop(0, qd, step, jnp.zeros((3 * na, 128), F32), unroll=8).astype(I32)
+    table = lax.fori_loop(0, qd // 2, step, jnp.zeros((3 * na, 128), F32), unroll=8)
+    midway()
+    table = lax.fori_loop(qd // 2, qd, step, table, unroll=8).astype(I32)
     offs = table[:na] + 128 * table[na : 2 * na]
     qs = table[2 * na :]
     for o in range(nbeam):
@@ -89,19 +91,16 @@
     return hi, (x - hi.astype(F32)).astype(BF16)
 
 
-def score(share, b0, nb, qd, req_ref, rows_ref, queries_ref, wq_ref, wc_ref, wx_ref, vec_ref, out_ref):
+def score(share, b0, nb, qd, twice_ref, rows_ref, queries_ref, wq_ref, wc_ref, wx_ref, vec_ref, out_ref):
     shards = wq_ref.shape[0]
     width = queries_ref.shape[1]
     m = nb * 2 * share
     qrows = []
-    dup = (iota((2 * share, share), 0) // 2 == iota((2 * share, share), 1)).astype(BF16)
     for i in range(nb):
         b = b0 + i
-        qvec = jnp.concatenate([req_ref[b, 2:3, :], req_ref[b, 3:4, : share - 128]], axis=1)
-        oht = (iota((qd, share), 0) == qvec).astype(F32).astype(BF16)
+        oht = (iota((qd, 2 * share), 0) == twice_ref[pl.ds(b, 1), :]).astype(F32).astype(BF16)
         qb = queries_ref[pl.ds(pl.multiple_of(b * qd, qd), qd), :]
-        qrow = lax.dot_general(oht, qb, TN, preferred_element_type=F32).astype(BF16)
-        qrows.append(jnp.dot(dup, qrow, preferred_element_type=F32).astype(BF16))
+        qrows.append(lax.dot_general(oht, qb, TN, preferred_element_type=F32).astype(BF16))
     qrow = jnp.concatenate(qrows, axis=0) if nb > 1 else qrows[0]
     child = rows_ref[...].reshape(m, width)
     cross = child * qrow
@@ -226,12 +225,15 @@
     wrecv,
     psend,
     precv,
+    fsend,
+    frecv,
 ):
     b, h = lax.axis_index("beam"), lax.axis_index("hid")
     core = lax.rem(b, 2)
     mate = b + 1 - 2 * core
     z = lax.rem(h, 2)
     across = h + 1 - 2 * z
+    beyond = lax.rem(b + BEAM // 2, BEAM)
     qd = ids.shape[0]
     half = table.shape[0] // 2
     depth = w_all.shape[2] // 2
@@ -248,6 +250,7 @@
     barrier = pltpu.get_barrier_semaphore()
     loop(1, BEAM, lambda j: pl.semaphore_signal(barrier, inc=1, device_id=(beam_peer(j), h), device_id_type=MESH))
     loop(1, HID, lambda j: pl.semaphore_signal(barrier, inc=1, device_id=(b, hid_peer(j)), device_id_type=MESH))
+    pl.semaphore_signal(barrier, inc=1, device_id=(beyond, across), device_id_type=MESH)
 
     def q_rows(i):
         return pl.ds(pl.multiple_of(i * qd, qd), qd)
@@ -265,13 +268,23 @@
         copy.start()
     for copy in own:
         copy.wait()
-    pl.semaphore_wait(barrier, BEAM + HID - 2)
+    pl.semaphore_wait(barrier, BEAM + HID - 1)
 
     def piece(shard, part):
         return w_all.at[shard, :, pl.ds(pl.multiple_of(part * depth, depth), depth), :]
 
     def w_copy(shard, to, slot):
         return remote(piece(shard, core), piece(shard, core), wsend.at[slot], wrecv.at[shard], (b, to))
+
+    def z_copy(shard):
+        return remote(piece(shard, core), piece(shard, core), wsend.at[0], wrecv.at[shard], (beyond, across))
+
+    def quarter(shard, side):
+        start = pl.multiple_of(core * depth + side * (depth // 2), depth // 2)
+        return w_all.at[shard, :, pl.ds(start, depth // 2), :]
+
+    def pass_on(shard, side, to):
+        return remote(quarter(shard, side), quarter(shard, side), fsend.at[side], frecv.at[side], (b, to))
 
     def mate_copy(shard):
         return remote(piece(shard, core), piece(shard, core), psend.at[shard], precv.at[shard], (mate, h))
@@ -289,38 +302,51 @@
     def r_copy(to, slot):
         return remote(req.at[to], req_all.at[slot], rsend.at[to], rrecv.at[slot], (to, h))
 
-    w_copy(h, across, 0).start()
+    z_copy(h).start()
     for j in range(1, 4):
         w_copy(h, x_peer(j), j).start()
     loop(1, HID, lambda j: v_copy(hid_peer(j), h).start())
     loop(1, BEAM, lambda j: q_copy(beam_peer(j), b).start())
 
-    route(h, BEAM, share, half, ids, req, rank, a_ref, c_ref, v0_ref, v1_ref, qi_ref)
+    def midway():
+        z_copy(across).wait_recv()
+        for j in (1, 3):
+            w_copy(across, x_peer(j), 3 + j).start()
+        mate_copy(across).start()
+
+    route(h, BEAM, share, half, midway, ids, req, rank, a_ref, c_ref, v0_ref, v1_ref, qi_ref)
     loop(1, BEAM, lambda j: r_copy(beam_peer(j), b).start())
     req_all[pl.ds(b, 1)] = req[pl.ds(b, 1)]
 
-    w_copy(across, across, 0).wait_recv()
-    for j in range(1, 4):
-        w_copy(across, x_peer(j), 3 + j).start()
-    mate_copy(across).start()
-
+
+    near = [lax.rem(across + 2 * j, HID) for j in (1, 3)]
+    far = lax.rem(across + 4, HID)
+    for j in (1, 3):
+        w_copy(x_peer(j), x_peer(j), 0).wait_recv()
+        mate_copy(x_peer(j)).start()
+    for side, shard in enumerate(near):
+        w_copy(shard, shard, 0).wait_recv()
+        pass_on(shard, side, x_peer(3 - 2 * side)).start()
+        mate_copy(shard).start()
+    w_copy(x_peer(2), x_peer(2), 0).wait_recv()
+    mate_copy(x_peer(2)).start()
+    for side in range(2):
+        pass_on(far, side, x_peer(3 - 2 * side)).wait_recv()
+    mate_copy(far).start()
     loop(1, BEAM, lambda j: r_copy(beam_peer(j), beam_peer(j)).wait_recv())
     for copy in pulls:
         copy.wait()
-
-    for j in range(1, 4):
-        for zz in (h, across):
-            shard = lax.rem(zz + 2 * j, HID)
-            w_copy(shard, shard, 0).wait_recv()
-            mate_copy(shard).start()
     loop(1, BEAM, lambda j: q_copy(beam_peer(j), beam_peer(j)).wait_recv())
     loop(1, HID, lambda j: v_copy(hid_peer(j), hid_peer(j)).wait_recv())
     loop(1, HID, lambda j: mate_arrival(hid_peer(j)).wait_recv())
 
-    w_copy(h, across, 0).wait_send()
+    z_copy(h).wait_send()
     for j in range(1, 4):
         w_copy(h, x_peer(j), j).wait_send()
+    for j in (1, 3):
         w_copy(across, x_peer(j), 3 + j).wait_send()
+    for side, shard in enumerate(near):
+        pass_on(shard, side, x_peer(3 - 2 * side)).wait_send()
     loop(1, BEAM, lambda j: q_copy(beam_peer(j), b).wait_send())
     loop(1, BEAM, lambda j: r_copy(beam_peer(j), b).wait_send())
     loop(1, HID, lambda j: v_copy(hid_peer(j), h).wait_send())
@@ -356,10 +382,15 @@
     loop(1, HID, lambda j: spread(hid_peer(j), hid_peer(j)).wait_recv())
 
 
-def score_kernel(share, nb, qd, req, off, queries, w_all, vec, buf, scores, rows):
+def score_kernel(share, nb, qd, req, off, queries, w_all, vec, buf, scores, rows, twice):
+    lists = req[...]
+    qs = jnp.concatenate([lists[:, 2, :], lists[:, 3, : share - 128]], axis=1).astype(F32).astype(BF16)
+    dup = (iota((share, 2 * share), 1) // 2 == iota((share, 2 * share), 0)).astype(F32).astype(BF16)
+    twice[...] = jnp.dot(qs, dup, preferred_element_type=F32).astype(I32)
+
     def step(i):
         gather(share, off, buf, rows, i * nb, nb)
-        score(share, i * nb, nb, qd, req, rows, queries, w_all.at[:, 0], w_all.at[:, 1], w_all.at[:, 2], vec, scores)
+        score(share, i * nb, nb, qd, twice, rows, queries, w_all.at[:, 0], w_all.at[:, 1], w_all.at[:, 2], vec, scores)
 
     loop(0, BEAM // nb, step)
 
@@ -378,7 +409,7 @@
         functools.partial(front_kernel, share),
         out_shape=(
             shape((qd, width), I32),
-            shape((BEAM, 4, 128), I32),
+            pltpu.VMEM((BEAM, 4, 128), I32),
             pltpu.VMEM((BEAM * qd, embed), BF16),
             pltpu.VMEM((HID, 3, embed, hid_dev), BF16),
             pltpu.VMEM((HID, 2, hid_dev), F32),
@@ -400,6 +431,7 @@
             dma(7),
             dma(HID),
             *[dma(HID)] * 2,
+            *[dma(2)] * 2,
         ],
         compiler_params=pltpu.CompilerParams(collective_id=0, has_side_effects=True, vmem_limit_bytes=45 * 2**20),
         name="front",
@@ -407,21 +439,21 @@
 
     scores = pl.pallas_call(
         functools.partial(score_kernel, share, nb, qd),
-        out_shape=shape((BEAM, 3, 128), F32),
+        out_shape=pltpu.VMEM((BEAM, 3, 128), F32),
         in_specs=[VM, pl.BlockSpec(memory_space=pltpu.SMEM)] + [VM] * 4,
         out_specs=VM,
-        scratch_shapes=[pltpu.VMEM((nb * share, 2, embed), BF16)],
+        scratch_shapes=[pltpu.VMEM((nb * share, 2, embed), BF16), pltpu.VMEM((BEAM, 2 * share), I32)],
         compiler_params=pltpu.CompilerParams(vmem_limit_bytes=20 * 2**20),
         name="score",
     )(req_all, req_all, q_all, w_all, vec_all, buf)
 
     sall = pl.pallas_call(
         back_kernel,
-        out_shape=shape((HID, BEAM, 3, 128), F32),
+        out_shape=pltpu.VMEM((HID, BEAM, 3, 128), F32),
         in_specs=[VM],
         out_specs=VM,
         scratch_shapes=[dma(BEAM), dma(BEAM), dma(HID), dma(HID)],
-        compiler_params=pltpu.CompilerParams(collective_id=1, has_side_effects=True),
+        compiler_params=pltpu.CompilerParams(collective_id=1, has_side_effects=True, vmem_limit_bytes=8 * 2**20),
         name="give_back",
     )(scores)
 
@@ -433,6 +465,7 @@
         out_shape=shape((qd, 2 * width // HID), F32),
         in_specs=[VM] * 3,
         out_specs=VM,
+        compiler_params=pltpu.CompilerParams(vmem_limit_bytes=56 * 2**20),
         name="place",
     )(beam_ids, rank, sall)
 

time: 64.5 us -> 60 us (0.930)
  Pallas kernels: 62.8 us -> 59.1 us
  local copies, waits for them, and re-layouts: 1.36 us -> 0.68 us
    pallas_call x1, Pallas kernels: 27.1 us -> 22.3 us  [shards(): pl.pallas_call(functools.partial(front_kernel, share), out_shape=(shape((...]
    pallas_call x1, Pallas kernels: 13.6 us -> 15.3 us  [shards(): pl.pallas_call(back_kernel, out_shape=pltpu.VMEM((HID, BEAM, 3, 128), F32...]
    unnamed x4 -> x2, local copies, waits for them, and re-layouts: 1.36 us -> 0.68 us
    pallas_call x1, Pallas kernels: 18.6 us -> 18 us  [shards(): pl.pallas_call(functools.partial(score_kernel, share, nb, qd), out_shape=...]
where the time goes in v4:
time: 60 us; the launch traced here: 59.8 us
  Pallas kernels  59.1 us (98%)
  local copies, waits for them, and re-layouts  0.68 us (1%)
    pallas_call x1, Pallas kernels, shards(): pl.pallas_call(functools.partial(front_kernel, share), out_shape=(shape((...  22.3 us
    pallas_call x1, Pallas kernels, shards(): pl.pallas_call(functools.partial(score_kernel, share, nb, qd), out_shape=...  18 us
    pallas_call x1, Pallas kernels, shards(): pl.pallas_call(back_kernel, out_shape=pltpu.VMEM((HID, BEAM, 3, 128), F32...  15.3 us
    pallas_call x1, Pallas kernels, shards(): pl.pallas_call(place_kernel, out_shape=shape((qd, 2 * width // HID), F32)...  3.53 us

profile of v4, /device:TPU:0, one launch (start us, length us, event | category | flops | bytes accessed | tf_op | source)
XLA Modules:
  0.0 59.8 jit_solution(16218569937226419661)
XLA Ops:
  0.0 22.3 %front.1 = (s32[64,256]{1,0:T(8,128)}, s32[16,4,128]{2,1,0:T(4,128)S(1)}, bf16[1024,256]{1,0:T(8,128)(2,1)S(1)}, bf16[8,3,256,128]{3,2,1,0:T(8,128)(2,1)S(1)}, f...) custom-call(s32[64,256]{1,0:T(8,128)} %ids.3, bf16[64,256]{1,0:T(8,128)(2,1)} %queries.1, ...), custom_call_target="tpu_custom_call" | custom-call | tf_op jit(solution)/shard_map/front/pallas_call | solution.py:408
  22.3 18.0 %score.1.scores = f32[16,3,128]{2,1,0:T(4,128)S(1)} custom-call(s32[16,4,128]{2,1,0:T(4,128)S(1)} %get-tuple-element.12.req.off, s32[16,4,128]{2,1,0:T(4,128)S(1)} %get-tuple-element.12.req.off, bf16[1024,256]{1,0:T(8,128)(2,1)S(1)} %get-tuple-element.13.queries, bf16[8,3,256,128]{3,2,1,0:T(8,128)(2,1)S(1)} %get-tuple-element.14.w_all, ...), custom_call_target="tpu_custom_call" | custom-call | tf_op jit(solution)/shard_map/score/pallas_call | solution.py:440
  40.3 15.3 %give_back.1.sall = f32[8,16,3,128]{3,2,1,0:T(4,128)S(1)} custom-call(f32[16,3,128]{2,1,0:T(4,128)S(1)} %score.1.scores), custom_call_target="tpu_custom_call" | custom-call | tf_op jit(solution)/shard_map/give_back/pallas_call | solution.py:450
  55.6 0.0 copy-start
  55.6 0.7 %copy-done = f32[8,16,3,128]{3,2,1,0:T(4,128)} copy-done((f32[8,16,3,128]{3,2,1,0:T(4,128)}, f32[8,16,3,128]{3,2,1,0:T(4,128)S(1)}, u32[]{:S(2)}) %copy-start) | copy-done | bytes 196632
  56.3 3.5 %place.1 = f32[64,64]{1,0:T(8,128)} custom-call(s32[64,256]{1,0:T(8,128)} %ids.3, s32[64,256]{1,0:T(8,128)} %get-tuple-element.11.rank, f32[8,16,3,128]{3,2,1,0:T(4,128)} %copy-done), custom_call_target="tpu_custom_call" | custom-call | tf_op jit(solution)/shard_map/place/pallas_call | solution.py:463
Async XLA Ops:
  55.6 0.7 %copy-start = (f32[8,16,3,128]{3,2,1,0:T(4,128)}, f32[8,16,3,128]{3,2,1,0:T(4,128)S(1)}, u32[]{:S(2)}) copy-start(f32[8,16,3,128]{3,2,1,0:T(4,128)S(1)} %give_back.1.sall) | copy-start | bytes 589828

commit v5 on v4

--- a/solution.py
+++ b/solution.py
@@ -78,12 +78,9 @@
 
 
 def gather(share, off_ref, buf_ref, rows_ref, first, count):
-    def one(b, _):
+    for i in range(count):
         for k in range(share):
-            rows_ref[b * share + k] = buf_ref[off_ref[first + b, k // 128, k % 128]]
-        return 0
-
-    lax.fori_loop(0, count, one, 0)
+            rows_ref[i * share + k] = buf_ref[off_ref[first + i, k // 128, k % 128]]
 
 
 def split2(x):
@@ -283,8 +280,13 @@
         start = pl.multiple_of(core * depth + side * (depth // 2), depth // 2)
         return w_all.at[shard, :, pl.ds(start, depth // 2), :]
 
-    def pass_on(shard, side, to):
-        return remote(quarter(shard, side), quarter(shard, side), fsend.at[side], frecv.at[side], (b, to))
+    def pass_on(shard, side, lane):
+        part = quarter(shard, side)
+        return remote(part, part, fsend.at[lane + side], frecv.at[lane + side], (b, x_peer(3 - 2 * side)))
+
+    beside = [x_peer(j) for j in (1, 3)]
+    near = [lax.rem(across + 2 * j, HID) for j in (1, 3)]
+    ends = (x_peer(2), lax.rem(across + 4, HID))
 
     def mate_copy(shard):
         return remote(piece(shard, core), piece(shard, core), psend.at[shard], precv.at[shard], (mate, h))
@@ -303,7 +305,7 @@
         return remote(req.at[to], req_all.at[slot], rsend.at[to], rrecv.at[slot], (to, h))
 
     z_copy(h).start()
-    for j in range(1, 4):
+    for j in (1, 3):
         w_copy(h, x_peer(j), j).start()
     loop(1, HID, lambda j: v_copy(hid_peer(j), h).start())
     loop(1, BEAM, lambda j: q_copy(beam_peer(j), b).start())
@@ -312,27 +314,26 @@
         z_copy(across).wait_recv()
         for j in (1, 3):
             w_copy(across, x_peer(j), 3 + j).start()
+        for side, shard in enumerate(beside):
+            w_copy(shard, shard, 0).wait_recv()
+            pass_on(shard, side, 0).start()
         mate_copy(across).start()
+        for shard in beside:
+            mate_copy(shard).start()
 
     route(h, BEAM, share, half, midway, ids, req, rank, a_ref, c_ref, v0_ref, v1_ref, qi_ref)
     loop(1, BEAM, lambda j: r_copy(beam_peer(j), b).start())
     req_all[pl.ds(b, 1)] = req[pl.ds(b, 1)]
 
 
-    near = [lax.rem(across + 2 * j, HID) for j in (1, 3)]
-    far = lax.rem(across + 4, HID)
-    for j in (1, 3):
-        w_copy(x_peer(j), x_peer(j), 0).wait_recv()
-        mate_copy(x_peer(j)).start()
     for side, shard in enumerate(near):
         w_copy(shard, shard, 0).wait_recv()
-        pass_on(shard, side, x_peer(3 - 2 * side)).start()
+        pass_on(shard, side, 2).start()
         mate_copy(shard).start()
-    w_copy(x_peer(2), x_peer(2), 0).wait_recv()
-    mate_copy(x_peer(2)).start()
-    for side in range(2):
-        pass_on(far, side, x_peer(3 - 2 * side)).wait_recv()
-    mate_copy(far).start()
+    for i, shard in enumerate(ends):
+        for side in range(2):
+            pass_on(shard, side, 2 * i).wait_recv()
+        mate_copy(shard).start()
     loop(1, BEAM, lambda j: r_copy(beam_peer(j), beam_peer(j)).wait_recv())
     for copy in pulls:
         copy.wait()
@@ -341,12 +342,12 @@
     loop(1, HID, lambda j: mate_arrival(hid_peer(j)).wait_recv())
 
     z_copy(h).wait_send()
-    for j in range(1, 4):
+    for j in (1, 3):
         w_copy(h, x_peer(j), j).wait_send()
-    for j in (1, 3):
         w_copy(across, x_peer(j), 3 + j).wait_send()
-    for side, shard in enumerate(near):
-        pass_on(shard, side, x_peer(3 - 2 * side)).wait_send()
+    for i, pair in enumerate((beside, near)):
+        for side, shard in enumerate(pair):
+            pass_on(shard, side, 2 * i).wait_send()
     loop(1, BEAM, lambda j: q_copy(beam_peer(j), b).wait_send())
     loop(1, BEAM, lambda j: r_copy(beam_peer(j), b).wait_send())
     loop(1, HID, lambda j: v_copy(hid_peer(j), h).wait_send())
@@ -382,17 +383,22 @@
     loop(1, HID, lambda j: spread(hid_peer(j), hid_peer(j)).wait_recv())
 
 
-def score_kernel(share, nb, qd, req, off, queries, w_all, vec, buf, scores, rows, twice):
+def score_kernel(share, nb, qd, req, off, queries, w_all, vec, buf, scores, rows, rows2, twice):
     lists = req[...]
     qs = jnp.concatenate([lists[:, 2, :], lists[:, 3, : share - 128]], axis=1).astype(F32).astype(BF16)
     dup = (iota((share, 2 * share), 1) // 2 == iota((share, 2 * share), 0)).astype(F32).astype(BF16)
     twice[...] = jnp.dot(qs, dup, preferred_element_type=F32).astype(I32)
 
+    def run(first, now, then):
+        gather(share, off, buf, then, jnp.minimum(first + nb, BEAM - nb), nb)
+        score(share, first, nb, qd, twice, now, queries, w_all.at[:, 0], w_all.at[:, 1], w_all.at[:, 2], vec, scores)
+
     def step(i):
-        gather(share, off, buf, rows, i * nb, nb)
-        score(share, i * nb, nb, qd, twice, rows, queries, w_all.at[:, 0], w_all.at[:, 1], w_all.at[:, 2], vec, scores)
-
-    loop(0, BEAM // nb, step)
+        run(2 * i * nb, rows, rows2)
+        run((2 * i + 1) * nb, rows2, rows)
+
+    gather(share, off, buf, rows, 0, nb)
+    loop(0, BEAM // (2 * nb), step)
 
 
 def shards(queries, beam_ids, child_table, w_query, w_child, w_cross, bias, w_out):
@@ -401,7 +407,7 @@
     half = child_table.shape[0] // 2
     hid_dev = w_query.shape[1]
     share = 3 * qd * width // (2 * BEAM * HID)
-    nb = 4
+    nb = 2
     ints = pltpu.VMEM((qd, width), I32)
     floats = pltpu.VMEM((qd, width), F32)
 
@@ -431,7 +437,7 @@
             dma(7),
             dma(HID),
             *[dma(HID)] * 2,
-            *[dma(2)] * 2,
+            *[dma(4)] * 2,
         ],
         compiler_params=pltpu.CompilerParams(collective_id=0, has_side_effects=True, vmem_limit_bytes=45 * 2**20),
         name="front",
@@ -442,7 +448,7 @@
         out_shape=pltpu.VMEM((BEAM, 3, 128), F32),
         in_specs=[VM, pl.BlockSpec(memory_space=pltpu.SMEM)] + [VM] * 4,
         out_specs=VM,
-        scratch_shapes=[pltpu.VMEM((nb * share, 2, embed), BF16), pltpu.VMEM((BEAM, 2 * share), I32)],
+        scratch_shapes=[*[pltpu.VMEM((nb * share, 2, embed), BF16)] * 2, pltpu.VMEM((BEAM, 2 * share), I32)],
         compiler_params=pltpu.CompilerParams(vmem_limit_bytes=20 * 2**20),
         name="score",
     )(req_all, req_all, q_all, w_all, vec_all, buf)
@@ -465,7 +471,7 @@
         out_shape=shape((qd, 2 * width // HID), F32),
         in_specs=[VM] * 3,
         out_specs=VM,
-        compiler_params=pltpu.CompilerParams(vmem_limit_bytes=56 * 2**20),
+        compiler_params=pltpu.CompilerParams(vmem_limit_bytes=24 * 2**20),
         name="place",
     )(beam_ids, rank, sall)
 

time: 60 us -> 56 us (0.933)
  Pallas kernels: 59.1 us -> 55.8 us
  local copies, waits for them, and re-layouts: 0.68 us -> 0.01 us
    pallas_call x1, Pallas kernels: 18 us -> 15.2 us  [shards(): pl.pallas_call(functools.partial(score_kernel, share, nb, qd), out_shape=...]
    pallas_call x1, Pallas kernels: 3.53 us -> 2.51 us  [shards(): pl.pallas_call(place_kernel, out_shape=shape((qd, 2 * width // HID), F32)...]
    unnamed x2 -> x4, local copies, waits for them, and re-layouts: 0.68 us -> 0.01 us
where the time goes in v5:
time: 56 us; the launch traced here: 55.8 us
  Pallas kernels  55.8 us (100%)
    pallas_call x1, Pallas kernels, shards(): pl.pallas_call(functools.partial(front_kernel, share), out_shape=(shape((...  22.7 us
    pallas_call x1, Pallas kernels, shards(): pl.pallas_call(back_kernel, out_shape=pltpu.VMEM((HID, BEAM, 3, 128), F32...  15.4 us
    pallas_call x1, Pallas kernels, shards(): pl.pallas_call(functools.partial(score_kernel, share, nb, qd), out_shape=...  15.2 us
    pallas_call x1, Pallas kernels, shards(): pl.pallas_call(place_kernel, out_shape=shape((qd, 2 * width // HID), F32)...  2.51 us

profile of v5, /device:TPU:0, one launch (start us, length us, event | category | flops | bytes accessed | tf_op | source)
XLA Modules:
  0.0 55.8 jit_solution(14228575963835464534)
XLA Ops:
  0.0 0.0 copy-start
  0.0 22.7 %front.1 = (s32[64,256]{1,0:T(8,128)}, s32[16,4,128]{2,1,0:T(4,128)S(1)}, bf16[1024,256]{1,0:T(8,128)(2,1)S(1)}, bf16[8,3,256,128]{3,2,1,0:T(8,128)(2,1)S(1)}, f...) custom-call(s32[64,256]{1,0:T(8,128)} %ids.3, bf16[64,256]{1,0:T(8,128)(2,1)} %queries.1, ...), custom_call_target="tpu_custom_call" | custom-call | tf_op jit(solution)/shard_map/front/pallas_call | solution.py:414
  22.7 0.0 copy-start.1
  22.8 15.2 %score.1.scores = f32[16,3,128]{2,1,0:T(4,128)S(1)} custom-call(s32[16,4,128]{2,1,0:T(4,128)S(1)} %get-tuple-element.12.req.off, s32[16,4,128]{2,1,0:T(4,128)S(1)} %get-tuple-element.12.req.off, bf16[1024,256]{1,0:T(8,128)(2,1)S(1)} %get-tuple-element.13.queries, bf16[8,3,256,128]{3,2,1,0:T(8,128)(2,1)S(1)} %get-tuple-element.14.w_all, ...), custom_call_target="tpu_custom_call" | custom-call | tf_op jit(solution)/shard_map/score/pallas_call | solution.py:446
  37.9 15.4 %give_back.1.sall = f32[8,16,3,128]{3,2,1,0:T(4,128)S(1)} custom-call(f32[16,3,128]{2,1,0:T(4,128)S(1)} %score.1.scores), custom_call_target="tpu_custom_call" | custom-call | tf_op jit(solution)/shard_map/give_back/pallas_call | solution.py:456
  53.3 0.0 copy-done
  53.3 0.0 copy-done.1
  53.3 2.5 %place.1 = f32[64,64]{1,0:T(8,128)} custom-call(s32[64,256]{1,0:T(8,128)S(1)} %copy-done, s32[64,256]{1,0:T(8,128)S(1)} %copy-done.1, f32[8,16,3,128]{3,2,1,0:T(4,128)S(1)} %give_back.1.sall), custom_call_target="tpu_custom_call" | custom-call | tf_op jit(solution)/shard_map/place/pallas_call | solution.py:469
Async XLA Ops:
  0.0 53.3 %copy-start = (s32[64,256]{1,0:T(8,128)S(1)}, s32[64,256]{1,0:T(8,128)}, u32[]{:S(2)}) copy-start(s32[64,256]{1,0:T(8,128)} %ids.3) | copy-start | bytes 196612
  22.7 30.6 %copy-start.1 = (s32[64,256]{1,0:T(8,128)S(1)}, s32[64,256]{1,0:T(8,128)}, u32[]{:S(2)}) copy-start(s32[64,256]{1,0:T(8,128)} %get-tuple-element.11.rank) | copy-start | bytes 196612

commit v6 on v5

--- a/solution.py
+++ b/solution.py
@@ -216,6 +216,7 @@
     rrecv,
     qsend,
     qrecv,
+    msend,
     vsend,
     vrecv,
     wsend,
@@ -298,6 +299,15 @@
     def q_copy(to, slot):
         return remote(q_all.at[q_rows(slot), :], q_all.at[q_rows(slot), :], qsend.at[to], qrecv.at[slot], (to, h))
 
+    def q_mate(slot):
+        return remote(q_all.at[q_rows(slot), :], q_all.at[q_rows(slot), :], msend.at[slot], qrecv.at[slot], (mate, h))
+
+    def twin(j):
+        return lax.rem(b + 2 * j, BEAM)
+
+    def mates_twin(j):
+        return lax.rem(mate + 2 * j, BEAM)
+
     def v_copy(to, slot):
         return remote(vec_all.at[slot], vec_all.at[slot], vsend.at[to], vrecv.at[slot], (b, to))
 
@@ -308,7 +318,8 @@
     for j in (1, 3):
         w_copy(h, x_peer(j), j).start()
     loop(1, HID, lambda j: v_copy(hid_peer(j), h).start())
-    loop(1, BEAM, lambda j: q_copy(beam_peer(j), b).start())
+    loop(1, BEAM // 2, lambda j: q_copy(twin(j), b).start())
+    q_mate(b).start()
 
     def midway():
         z_copy(across).wait_recv()
@@ -324,6 +335,12 @@
     route(h, BEAM, share, half, midway, ids, req, rank, a_ref, c_ref, v0_ref, v1_ref, qi_ref)
     loop(1, BEAM, lambda j: r_copy(beam_peer(j), b).start())
     req_all[pl.ds(b, 1)] = req[pl.ds(b, 1)]
+
+    def hand_over(j):
+        q_copy(twin(j), twin(j)).wait_recv()
+        q_mate(twin(j)).start()
+
+    loop(1, BEAM // 2, hand_over)
 
 
     for side, shard in enumerate(near):
@@ -337,7 +354,7 @@
     loop(1, BEAM, lambda j: r_copy(beam_peer(j), beam_peer(j)).wait_recv())
     for copy in pulls:
         copy.wait()
-    loop(1, BEAM, lambda j: q_copy(beam_peer(j), beam_peer(j)).wait_recv())
+    loop(0, BEAM // 2, lambda j: q_mate(mates_twin(j)).wait_recv())
     loop(1, HID, lambda j: v_copy(hid_peer(j), hid_peer(j)).wait_recv())
     loop(1, HID, lambda j: mate_arrival(hid_peer(j)).wait_recv())
 
@@ -348,7 +365,8 @@
     for i, pair in enumerate((beside, near)):
         for side, shard in enumerate(pair):
             pass_on(shard, side, 2 * i).wait_send()
-    loop(1, BEAM, lambda j: q_copy(beam_peer(j), b).wait_send())
+    loop(1, BEAM // 2, lambda j: q_copy(twin(j), b).wait_send())
+    loop(0, BEAM // 2, lambda j: q_mate(twin(j)).wait_send())
     loop(1, BEAM, lambda j: r_copy(beam_peer(j), b).wait_send())
     loop(1, HID, lambda j: v_copy(hid_peer(j), h).wait_send())
     loop(1, HID, lambda j: mate_copy(hid_peer(j)).wait_send())
@@ -432,7 +450,7 @@
             floats,
             dma(4),
             dma(6),
-            *[dma(BEAM)] * 4,
+            *[dma(BEAM)] * 5,
             *[dma(HID)] * 2,
             dma(7),
             dma(HID),

time: 56 us -> 56 us (level)
  no operation moved by 1% of the time
where the time goes in v6:
time: 56 us; the launch traced here: 55.9 us
  Pallas kernels  55.8 us (100%)
    pallas_call x1, Pallas kernels, shards(): pl.pallas_call(functools.partial(front_kernel, share), out_shape=(shape((...  22.9 us
    pallas_call x1, Pallas kernels, shards(): pl.pallas_call(back_kernel, out_shape=pltpu.VMEM((HID, BEAM, 3, 128), F32...  15.3 us
    pallas_call x1, Pallas kernels, shards(): pl.pallas_call(functools.partial(score_kernel, share, nb, qd), out_shape=...  15.2 us
    pallas_call x1, Pallas kernels, shards(): pl.pallas_call(place_kernel, out_shape=shape((qd, 2 * width // HID), F32)...  2.51 us

profile of v6, /device:TPU:0, one launch (start us, length us, event | category | flops | bytes accessed | tf_op | source)
XLA Modules:
  0.0 55.9 jit_solution(5304447561021147711)
XLA Ops:
  0.0 0.0 copy-start
  0.0 22.9 %front.1 = (s32[64,256]{1,0:T(8,128)}, s32[16,4,128]{2,1,0:T(4,128)S(1)}, bf16[1024,256]{1,0:T(8,128)(2,1)S(1)}, bf16[8,3,256,128]{3,2,1,0:T(8,128)(2,1)S(1)}, f...) custom-call(s32[64,256]{1,0:T(8,128)} %ids.3, bf16[64,256]{1,0:T(8,128)(2,1)} %queries.1, ...), custom_call_target="tpu_custom_call" | custom-call | tf_op jit(solution)/shard_map/front/pallas_call | solution.py:432
  22.9 0.0 copy-start.1
  22.9 15.2 %score.1.scores = f32[16,3,128]{2,1,0:T(4,128)S(1)} custom-call(s32[16,4,128]{2,1,0:T(4,128)S(1)} %get-tuple-element.12.req.off, s32[16,4,128]{2,1,0:T(4,128)S(1)} %get-tuple-element.12.req.off, bf16[1024,256]{1,0:T(8,128)(2,1)S(1)} %get-tuple-element.13.queries, bf16[8,3,256,128]{3,2,1,0:T(8,128)(2,1)S(1)} %get-tuple-element.14.w_all, ...), custom_call_target="tpu_custom_call" | custom-call | tf_op jit(solution)/shard_map/score/pallas_call | solution.py:464
  38.0 15.3 %give_back.1.sall = f32[8,16,3,128]{3,2,1,0:T(4,128)S(1)} custom-call(f32[16,3,128]{2,1,0:T(4,128)S(1)} %score.1.scores), custom_call_target="tpu_custom_call" | custom-call | tf_op jit(solution)/shard_map/give_back/pallas_call | solution.py:474
  53.4 0.0 copy-done
  53.4 0.0 copy-done.1
  53.4 2.5 %place.1 = f32[64,64]{1,0:T(8,128)} custom-call(s32[64,256]{1,0:T(8,128)S(1)} %copy-done, s32[64,256]{1,0:T(8,128)S(1)} %copy-done.1, f32[8,16,3,128]{3,2,1,0:T(4,128)S(1)} %give_back.1.sall), custom_call_target="tpu_custom_call" | custom-call | tf_op jit(solution)/shard_map/place/pallas_call | solution.py:487
Async XLA Ops:
  0.0 53.4 %copy-start = (s32[64,256]{1,0:T(8,128)S(1)}, s32[64,256]{1,0:T(8,128)}, u32[]{:S(2)}) copy-start(s32[64,256]{1,0:T(8,128)} %ids.3) | copy-start | bytes 196612
  22.9 30.5 %copy-start.1 = (s32[64,256]{1,0:T(8,128)S(1)}, s32[64,256]{1,0:T(8,128)}, u32[]{:S(2)}) copy-start(s32[64,256]{1,0:T(8,128)} %get-tuple-element.11.rank) | copy-start | bytes 196612

commit v7 on v6

--- a/solution.py
+++ b/solution.py
@@ -17,7 +17,7 @@
     return lax.broadcasted_iota(I32, shape, dim)
 
 
-def route(h, nbeam, share, half, midway, ids_ref, req_ref, rank_ref, a_ref, c_ref, v0_ref, v1_ref, q_ref):
+def route(h, nbeam, share, half, ranked, midway, ids_ref, req_ref, rank_ref, a_ref, c_ref, v0_ref, v1_ref, q_ref):
     qd, width = ids_ref.shape
     lo = ids_ref[:, :128]
     hi = ids_ref[:, 128:]
@@ -37,6 +37,7 @@
     rank = rank.astype(I32)
     rank = jnp.concatenate([rank[:qd], rank[qd:]], axis=1)
     rank_ref[...] = rank
+    ranked()
     ids = ids_ref[...]
     owner = ids // half
     offset = ids - owner * half
@@ -264,10 +265,6 @@
     pulls = table_copies(table, buf, table_sem)
     for copy in pulls:
         copy.start()
-    for copy in own:
-        copy.wait()
-    pl.semaphore_wait(barrier, BEAM + HID - 1)
-
     def piece(shard, part):
         return w_all.at[shard, :, pl.ds(pl.multiple_of(part * depth, depth), depth), :]
 
@@ -314,27 +311,31 @@
     def r_copy(to, slot):
         return remote(req.at[to], req_all.at[slot], rsend.at[to], rrecv.at[slot], (to, h))
 
-    z_copy(h).start()
-    for j in (1, 3):
-        w_copy(h, x_peer(j), j).start()
-    loop(1, HID, lambda j: v_copy(hid_peer(j), h).start())
-    loop(1, BEAM // 2, lambda j: q_copy(twin(j), b).start())
-    q_mate(b).start()
+    def ranked():
+        for copy in own:
+            copy.wait()
+        pl.semaphore_wait(barrier, BEAM + HID - 1)
+        z_copy(h).start()
+        for j in (1, 3):
+            w_copy(h, x_peer(j), j).start()
+        loop(1, HID, lambda j: v_copy(hid_peer(j), h).start())
+        loop(1, BEAM // 2, lambda j: q_copy(twin(j), b).start())
+        q_mate(b).start()
 
     def midway():
         z_copy(across).wait_recv()
         for j in (1, 3):
             w_copy(across, x_peer(j), 3 + j).start()
-        for side, shard in enumerate(beside):
-            w_copy(shard, shard, 0).wait_recv()
-            pass_on(shard, side, 0).start()
         mate_copy(across).start()
-        for shard in beside:
-            mate_copy(shard).start()
-
-    route(h, BEAM, share, half, midway, ids, req, rank, a_ref, c_ref, v0_ref, v1_ref, qi_ref)
+
+    route(h, BEAM, share, half, ranked, midway, ids, req, rank, a_ref, c_ref, v0_ref, v1_ref, qi_ref)
     loop(1, BEAM, lambda j: r_copy(beam_peer(j), b).start())
     req_all[pl.ds(b, 1)] = req[pl.ds(b, 1)]
+
+    for side, shard in enumerate(beside):
+        w_copy(shard, shard, 0).wait_recv()
+        pass_on(shard, side, 0).start()
+        mate_copy(shard).start()
 
     def hand_over(j):
         q_copy(twin(j), twin(j)).wait_recv()

time: 56 us -> 55.3 us (0.987)
  Pallas kernels: 55.8 us -> 55.1 us
    pallas_call x1, Pallas kernels: 15.3 us -> 14.4 us  [shards(): pl.pallas_call(back_kernel, out_shape=pltpu.VMEM((HID, BEAM, 3, 128), F32...]
where the time goes in v7:
time: 55.3 us; the launch traced here: 55.1 us
  Pallas kernels  55.1 us (100%)
    pallas_call x1, Pallas kernels, shards(): pl.pallas_call(functools.partial(front_kernel, share), out_shape=(shape((...  23 us
    pallas_call x1, Pallas kernels, shards(): pl.pallas_call(functools.partial(score_kernel, share, nb, qd), out_shape=...  15.1 us
    pallas_call x1, Pallas kernels, shards(): pl.pallas_call(back_kernel, out_shape=pltpu.VMEM((HID, BEAM, 3, 128), F32...  14.4 us
    pallas_call x1, Pallas kernels, shards(): pl.pallas_call(place_kernel, out_shape=shape((qd, 2 * width // HID), F32)...  2.51 us

profile of v7, /device:TPU:0, one launch (start us, length us, event | category | flops | bytes accessed | tf_op | source)
XLA Modules:
  0.0 55.1 jit_solution(13358262568663811663)
XLA Ops:
  0.0 0.0 copy-start
  0.0 23.0 %front.1 = (s32[64,256]{1,0:T(8,128)}, s32[16,4,128]{2,1,0:T(4,128)S(1)}, bf16[1024,256]{1,0:T(8,128)(2,1)S(1)}, bf16[8,3,256,128]{3,2,1,0:T(8,128)(2,1)S(1)}, f...) custom-call(s32[64,256]{1,0:T(8,128)} %ids.3, bf16[64,256]{1,0:T(8,128)(2,1)} %queries.1, ...), custom_call_target="tpu_custom_call" | custom-call | tf_op jit(solution)/shard_map/front/pallas_call | solution.py:433
  23.0 0.0 copy-start.1
  23.0 15.1 %score.1.scores = f32[16,3,128]{2,1,0:T(4,128)S(1)} custom-call(s32[16,4,128]{2,1,0:T(4,128)S(1)} %get-tuple-element.12.req.off, s32[16,4,128]{2,1,0:T(4,128)S(1)} %get-tuple-element.12.req.off, bf16[1024,256]{1,0:T(8,128)(2,1)S(1)} %get-tuple-element.13.queries, bf16[8,3,256,128]{3,2,1,0:T(8,128)(2,1)S(1)} %get-tuple-element.14.w_all, ...), custom_call_target="tpu_custom_call" | custom-call | tf_op jit(solution)/shard_map/score/pallas_call | solution.py:465
  38.1 14.4 %give_back.1.sall = f32[8,16,3,128]{3,2,1,0:T(4,128)S(1)} custom-call(f32[16,3,128]{2,1,0:T(4,128)S(1)} %score.1.scores), custom_call_target="tpu_custom_call" | custom-call | tf_op jit(solution)/shard_map/give_back/pallas_call | solution.py:475
  52.6 0.0 copy-done
  52.6 0.0 copy-done.1
  52.6 2.5 %place.1 = f32[64,64]{1,0:T(8,128)} custom-call(s32[64,256]{1,0:T(8,128)S(1)} %copy-done, s32[64,256]{1,0:T(8,128)S(1)} %copy-done.1, f32[8,16,3,128]{3,2,1,0:T(4,128)S(1)} %give_back.1.sall), custom_call_target="tpu_custom_call" | custom-call | tf_op jit(solution)/shard_map/place/pallas_call | solution.py:488
Async XLA Ops:
  0.0 52.6 %copy-start = (s32[64,256]{1,0:T(8,128)S(1)}, s32[64,256]{1,0:T(8,128)}, u32[]{:S(2)}) copy-start(s32[64,256]{1,0:T(8,128)} %ids.3) | copy-start | bytes 196612
  23.0 29.6 %copy-start.1 = (s32[64,256]{1,0:T(8,128)S(1)}, s32[64,256]{1,0:T(8,128)}, u32[]{:S(2)}) copy-start(s32[64,256]{1,0:T(8,128)} %get-tuple-element.11.rank) | copy-start | bytes 196612

commit v8 on v7

--- a/solution.py
+++ b/solution.py
@@ -116,7 +116,7 @@
     for i in range(nb):
         for t in range(2 * share // 128):
             lo = i * 2 * share + t * 128
-            out_ref[b0 + i, t : t + 1, :] = total[:, lo : lo + 128]
+            out_ref[pl.ds((b0 + i) * (2 * share // 128) + t, 1), :] = total[:, lo : lo + 128]
 
 
 def unpermute(h, nhid, nbeam, share, half, ids_ref, rank_ref, sall_ref, out_ref):
@@ -191,7 +191,7 @@
 
 def front_kernel(
     share,
-    ids,
+    ids_hbm,
     queries,
     wq,
     wc,
@@ -205,6 +205,7 @@
     w_all,
     vec_all,
     buf,
+    ids,
     req,
     a_ref,
     c_ref,
@@ -246,6 +247,8 @@
     def x_peer(j):
         return lax.rem(h + 2 * j, HID)
 
+    ids_copy = pltpu.make_async_copy(ids_hbm, ids, own_sem.at[6])
+    ids_copy.start()
     barrier = pltpu.get_barrier_semaphore()
     loop(1, BEAM, lambda j: pl.semaphore_signal(barrier, inc=1, device_id=(beam_peer(j), h), device_id_type=MESH))
     loop(1, HID, lambda j: pl.semaphore_signal(barrier, inc=1, device_id=(b, hid_peer(j)), device_id_type=MESH))
@@ -328,6 +331,7 @@
             w_copy(across, x_peer(j), 3 + j).start()
         mate_copy(across).start()
 
+    ids_copy.wait()
     route(h, BEAM, share, half, ranked, midway, ids, req, rank, a_ref, c_ref, v0_ref, v1_ref, qi_ref)
     loop(1, BEAM, lambda j: r_copy(beam_peer(j), b).start())
     req_all[pl.ds(b, 1)] = req[pl.ds(b, 1)]
@@ -375,6 +379,10 @@
 
 def back_kernel(scores, sall, bsend, brecv, hsend, hrecv):
     b, h = lax.axis_index("beam"), lax.axis_index("hid")
+    tiles = scores.shape[0] // BEAM
+
+    def lists(i):
+        return pl.ds(i * tiles, tiles)
 
     def beam_peer(j):
         return lax.rem(b + j, BEAM)
@@ -388,13 +396,14 @@
     pl.semaphore_wait(barrier, BEAM + HID - 2)
 
     def back(to, slot):
-        return remote(scores.at[to], sall.at[h, slot], bsend.at[to], brecv.at[slot], (to, h))
+        return remote(scores.at[lists(to), :], sall.at[h, lists(slot), :], bsend.at[to], brecv.at[slot], (to, h))
 
     def spread(to, slot):
         return remote(sall.at[slot], sall.at[slot], hsend.at[to], hrecv.at[slot], (b, to))
 
     loop(1, BEAM, lambda j: back(beam_peer(j), b).start())
-    sall[h, pl.ds(b, 1)] = scores[pl.ds(b, 1)]
+    for t in range(tiles):
+        sall[h, pl.ds(b * tiles + t, 1), :] = scores[pl.ds(b * tiles + t, 1), :]
     loop(1, BEAM, lambda j: back(beam_peer(j), beam_peer(j)).wait_recv())
     loop(1, HID, lambda j: spread(hid_peer(j), h).start())
     loop(1, BEAM, lambda j: back(beam_peer(j), b).wait_send())
@@ -427,22 +436,24 @@
     hid_dev = w_query.shape[1]
     share = 3 * qd * width // (2 * BEAM * HID)
     nb = 2
+    tiles = 2 * share // 128
     ints = pltpu.VMEM((qd, width), I32)
     floats = pltpu.VMEM((qd, width), F32)
 
     rank, req_all, q_all, w_all, vec_all, buf = pl.pallas_call(
         functools.partial(front_kernel, share),
         out_shape=(
-            shape((qd, width), I32),
+            pltpu.VMEM((qd, width), I32),
             pltpu.VMEM((BEAM, 4, 128), I32),
             pltpu.VMEM((BEAM * qd, embed), BF16),
             pltpu.VMEM((HID, 3, embed, hid_dev), BF16),
             pltpu.VMEM((HID, 2, hid_dev), F32),
             pltpu.VMEM((half, 2, embed), BF16),
         ),
-        in_specs=[VM] + [ANY] * 7,
+        in_specs=[ANY] * 8,
         out_specs=(VM,) * 6,
         scratch_shapes=[
+            ints,
             pltpu.VMEM((BEAM, 4, 128), I32),
             ints,
             ints,
@@ -450,7 +461,7 @@
             floats,
             floats,
             dma(4),
-            dma(6),
+            dma(7),
             *[dma(BEAM)] * 5,
             *[dma(HID)] * 2,
             dma(7),
@@ -464,7 +475,7 @@
 
     scores = pl.pallas_call(
         functools.partial(score_kernel, share, nb, qd),
-        out_shape=pltpu.VMEM((BEAM, 3, 128), F32),
+        out_shape=pltpu.VMEM((BEAM * tiles, 128), F32),
         in_specs=[VM, pl.BlockSpec(memory_space=pltpu.SMEM)] + [VM] * 4,
         out_specs=VM,
         scratch_shapes=[*[pltpu.VMEM((nb * share, 2, embed), BF16)] * 2, pltpu.VMEM((BEAM, 2 * share), I32)],
@@ -474,7 +485,7 @@
 
     sall = pl.pallas_call(
         back_kernel,
-        out_shape=pltpu.VMEM((HID, BEAM, 3, 128), F32),
+        out_shape=pltpu.VMEM((HID, BEAM * tiles, 128), F32),
         in_specs=[VM],
         out_specs=VM,
         scratch_shapes=[dma(BEAM), dma(BEAM), dma(HID), dma(HID)],

time: 55.3 us -> 54.5 us (0.986)
  Pallas kernels: 55.1 us -> 54.4 us
    pallas_call x2, Pallas kernels: 37.4 us -> 36.8 us  [the longest x1 21.7 us: shards(): pl.pallas_call(functools.partial(front_kernel, share), out_shape=(pltpu.V...]
where the time goes in v8:
time: 54.5 us; the launch traced here: 54.4 us
  Pallas kernels  54.4 us (100%)
    pallas_call x1, Pallas kernels, shards(): pl.pallas_call(functools.partial(front_kernel, share), out_shape=(pltpu.V...  21.7 us
    pallas_call x1, Pallas kernels, shards(): pl.pallas_call(functools.partial(score_kernel, share, nb, qd), out_shape=...  15.1 us
    pallas_call x1, Pallas kernels, shards(): pl.pallas_call(back_kernel, out_shape=pltpu.VMEM((HID, BEAM * tiles, 128)...  15.1 us
    pallas_call x1, Pallas kernels, shards(): pl.pallas_call(place_kernel, out_shape=shape((qd, 2 * width // HID), F32)...  2.46 us

profile of v8, /device:TPU:0, one launch (start us, length us, event | category | flops | bytes accessed | tf_op | source)
XLA Modules:
  0.0 54.4 jit_solution(1952526641982343804)
XLA Ops:
  0.0 0.0 copy-start
  0.0 21.7 %front.1 = (s32[64,256]{1,0:T(8,128)S(1)}, s32[16,4,128]{2,1,0:T(4,128)S(1)}, bf16[1024,256]{1,0:T(8,128)(2,1)S(1)}, bf16[8,3,256,128]{3,2,1,0:T(8,128)(2,1)S(1)...) custom-call(s32[64,256]{1,0:T(8,128)} %ids.1, bf16[64,256]{1,0:T(8,128)(2,1)} %queries.1, ...), custom_call_target="tpu_custom_call" | custom-call | tf_op jit(solution)/shard_map/front/pallas_call | solution.py:443
  21.7 15.1 %score.1.scores = f32[48,128]{1,0:T(8,128)S(1)} custom-call(s32[16,4,128]{2,1,0:T(4,128)S(1)} %get-tuple-element.12.req.off, s32[16,4,128]{2,1,0:T(4,128)S(1)} %get-tuple-element.12.req.off, bf16[1024,256]{1,0:T(8,128)(2,1)S(1)} %get-tuple-element.13.queries, bf16[8,3,256,128]{3,2,1,0:T(8,128)(2,1)S(1)} %get-tuple-element.14.w_all, ...), custom_call_target="tpu_custom_call" | custom-call | tf_op jit(solution)/shard_map/score/pallas_call | solution.py:476
  36.9 15.1 %give_back.1.sall = f32[8,48,128]{2,1,0:T(8,128)S(1)} custom-call(f32[48,128]{1,0:T(8,128)S(1)} %score.1.scores), custom_call_target="tpu_custom_call" | custom-call | tf_op jit(solution)/shard_map/give_back/pallas_call | solution.py:486
  51.9 0.0 copy-done
  52.0 2.5 %place.1 = f32[64,64]{1,0:T(8,128)} custom-call(s32[64,256]{1,0:T(8,128)S(1)} %copy-done, s32[64,256]{1,0:T(8,128)S(1)} %get-tuple-element.11.rank, f32[8,48,128]{2,1,0:T(8,128)S(1)} %give_back.1.sall), custom_call_target="tpu_custom_call" | custom-call | tf_op jit(solution)/shard_map/place/pallas_call | solution.py:499
Async XLA Ops:
  0.0 51.9 %copy-start = (s32[64,256]{1,0:T(8,128)S(1)}, s32[64,256]{1,0:T(8,128)}, u32[]{:S(2)}) copy-start(s32[64,256]{1,0:T(8,128)} %ids.1) | copy-start | bytes 196612

commit v9 on v8

--- a/solution.py
+++ b/solution.py
@@ -60,9 +60,9 @@
         right = (crow == c_ref[one, :]).astype(F32)
         return total + lax.dot_general(left.astype(BF16), right.astype(BF16), NT, preferred_element_type=F32)
 
-    table = lax.fori_loop(0, qd // 2, step, jnp.zeros((3 * na, 128), F32), unroll=8)
+    table = lax.fori_loop(0, qd // 2, step, jnp.zeros((3 * na, 128), F32), unroll=16)
     midway()
-    table = lax.fori_loop(qd // 2, qd, step, table, unroll=8).astype(I32)
+    table = lax.fori_loop(qd // 2, qd, step, table, unroll=16).astype(I32)
     offs = table[:na] + 128 * table[na : 2 * na]
     qs = table[2 * na :]
     for o in range(nbeam):

time: 54.5 us -> 54.1 us (level)
  no operation moved by 1% of the time
where the time goes in v9:
time: 54.1 us; the launch traced here: 54 us
  Pallas kernels  53.9 us (100%)
    pallas_call x1, Pallas kernels, shards(): pl.pallas_call(functools.partial(front_kernel, share), out_shape=(pltpu.V...  21.5 us
    pallas_call x1, Pallas kernels, shards(): pl.pallas_call(functools.partial(score_kernel, share, nb, qd), out_shape=...  15.2 us
    pallas_call x1, Pallas kernels, shards(): pl.pallas_call(back_kernel, out_shape=pltpu.VMEM((HID, BEAM * tiles, 128)...  14.8 us
    pallas_call x1, Pallas kernels, shards(): pl.pallas_call(place_kernel, out_shape=shape((qd, 2 * width // HID), F32)...  2.46 us

profile of v9, /device:TPU:0, one launch (start us, length us, event | category | flops | bytes accessed | tf_op | source)
XLA Modules:
  0.0 54.0 jit_solution(5600959846404815314)
XLA Ops:
  0.0 0.0 copy-start
  0.0 21.5 %front.1 = (s32[64,256]{1,0:T(8,128)S(1)}, s32[16,4,128]{2,1,0:T(4,128)S(1)}, bf16[1024,256]{1,0:T(8,128)(2,1)S(1)}, bf16[8,3,256,128]{3,2,1,0:T(8,128)(2,1)S(1)...) custom-call(s32[64,256]{1,0:T(8,128)} %ids.1, bf16[64,256]{1,0:T(8,128)(2,1)} %queries.1, ...), custom_call_target="tpu_custom_call" | custom-call | tf_op jit(solution)/shard_map/front/pallas_call | solution.py:443
  21.5 15.2 %score.1.scores = f32[48,128]{1,0:T(8,128)S(1)} custom-call(s32[16,4,128]{2,1,0:T(4,128)S(1)} %get-tuple-element.12.req.off, s32[16,4,128]{2,1,0:T(4,128)S(1)} %get-tuple-element.12.req.off, bf16[1024,256]{1,0:T(8,128)(2,1)S(1)} %get-tuple-element.13.queries, bf16[8,3,256,128]{3,2,1,0:T(8,128)(2,1)S(1)} %get-tuple-element.14.w_all, ...), custom_call_target="tpu_custom_call" | custom-call | tf_op jit(solution)/shard_map/score/pallas_call | solution.py:476
  36.7 14.8 %give_back.1.sall = f32[8,48,128]{2,1,0:T(8,128)S(1)} custom-call(f32[48,128]{1,0:T(8,128)S(1)} %score.1.scores), custom_call_target="tpu_custom_call" | custom-call | tf_op jit(solution)/shard_map/give_back/pallas_call | solution.py:486
  51.5 0.0 copy-done
  51.5 2.5 %place.1 = f32[64,64]{1,0:T(8,128)} custom-call(s32[64,256]{1,0:T(8,128)S(1)} %copy-done, s32[64,256]{1,0:T(8,128)S(1)} %get-tuple-element.11.rank, f32[8,48,128]{2,1,0:T(8,128)S(1)} %give_back.1.sall), custom_call_target="tpu_custom_call" | custom-call | tf_op jit(solution)/shard_map/place/pallas_call | solution.py:499
Async XLA Ops:
  0.0 51.5 %copy-start = (s32[64,256]{1,0:T(8,128)S(1)}, s32[64,256]{1,0:T(8,128)}, u32[]{:S(2)}) copy-start(s32[64,256]{1,0:T(8,128)} %ids.1) | copy-start | bytes 196612
